TPU v7x, 32 devices: a whole 2x2x4 slice. The times are simulated.
32 devices in a mesh: band: 4 (over z), ga: 8 (over y, x, core).
Axes of the slice: x: 2, y: 2, z: 4, core: 2. Of those that a mesh axis runs over, the one named last changes fastest.
Arguments:
- waves: bfloat16 [2, 128, 8192], P(None, 'band', 'ga'), may hold values from -6 to 6
- occupations: float32 [128], P('band'), may hold values from 0.0015625 to 0.03125
- beta_table: float32 [72, 8192], P(None, 'ga'), may hold values from -0.046875 to 0.046875
- wave_miller: int32 [3, 8192], P(None, 'ga'), may hold values from 0 to 223
- atom_kinds: int32 [256], replicated, may hold values from 0 to 3
- atom_sites: int32 [3, 256], replicated, may hold values from 0 to 223
- aug_table: bfloat16 [684, 57344], P(None, ('band', 'ga')), may hold values from -0.00061035156 to 0.00061035156
- stick_columns: int32 [256], P(('band', 'ga')), may hold values from -1 to 14399, as said below
Outputs:
- density: float32 [2, 224, 240, 240], P(None, 'ga', 'band')
Inputs may be any that keep to these rules, and one draw needn't show every extreme that they name: `stick_columns`: entry t is a slot of the device at place t // 8 in band-major order, of band index t // 64. -1 marks an empty slot; otherwise the entry c names the column x = (t // 64) * 60 + c // 240, y = c mod 240. Live columns of one band index are distinct. On each device the live slots come first and at least one is live; in each band index some device has all 8 slots live.
All inputs are finite; a program needn't handle non-finite values.
Results may differ from a plain program's by a relative error of at most 0.0035.
Values sent between devices are 32-bit elements; how exact they have to be, the bound alone decides.
A program may use at most 64 MiB of HBM per device.

v0:
```python
import math

import jax
import jax.numpy as jnp
import numpy as np
from jax import lax
from jax.sharding import PartitionSpec as P

NX = 240
NY = 240
NZ = 224
NH = 18
SPECIES = 4
ATOMS = 256


highest = lax.Precision.HIGHEST


def pair_tables(proj_count):
    ell_values = np.array([0, 0] + [1] * 6 + [2] * 10)
    pair_first, pair_second = np.triu_indices(proj_count)
    factors = np.where(pair_first == pair_second, 1.0, 2.0).astype(np.float32)
    parity = ((ell_values[pair_first] + ell_values[pair_second]) % 2).astype(np.float32)
    return (pair_first * proj_count + pair_second, factors, parity)


def phase_coefficients():
    ell_values = np.array([0, 0] + [1] * 6 + [2] * 10)
    coef_real = np.array([1.0, 0.0, -1.0])[ell_values]
    coef_imag = np.array([0.0, -1.0, 0.0])[ell_values]
    return (jnp.asarray(coef_real, jnp.float32), jnp.asarray(coef_imag, jnp.float32))


def phase_angle(site_block, first, second, third):
    turn_count = site_block[0][:, None] * first[None, :] % NX * (NY * NZ)
    turn_count = turn_count + site_block[1][:, None] * second[None, :] % NY * (NX * NZ)
    turn_count = turn_count + site_block[2][:, None] * third[None, :] % NZ * (NX * NY)
    turn_count = turn_count % (NX * NY * NZ)
    angle_value = turn_count.astype(jnp.float32) * (2.0 * np.pi / (NX * NY * NZ))
    return (jnp.cos(angle_value), -jnp.sin(angle_value))


def projector_rows(site_block, kinds_block, beta_table, wave_miller):
    struct_re, struct_im = phase_angle(site_block, wave_miller[0], wave_miller[1], wave_miller[2])
    kind_onehot = (kinds_block[:, None] == jnp.arange(SPECIES, dtype=jnp.int32)[None, :]).astype(
        jnp.float32
    )
    table_three = beta_table.reshape(SPECIES, NH, -1)
    radial = jnp.einsum("as,sig->aig", kind_onehot, table_three, precision=highest)
    coef_real, coef_imag = phase_coefficients()
    part_re = radial * struct_re[:, None, :]
    part_im = radial * struct_im[:, None, :]
    vkb_re = coef_real[None, :, None] * part_re - coef_imag[None, :, None] * part_im
    vkb_im = coef_real[None, :, None] * part_im + coef_imag[None, :, None] * part_re
    return (vkb_re.astype(jnp.bfloat16), vkb_im.astype(jnp.bfloat16))


def augment_weights(becsum, atom_kinds):
    pair_index, factors, parity = pair_tables(NH)
    kind_onehot = (atom_kinds[None, :] == jnp.arange(SPECIES, dtype=jnp.int32)[:, None]).astype(
        jnp.float32
    )
    parity_col = jnp.asarray(parity, jnp.float32)[:, None]
    even_rows = becsum.T * (1.0 - parity_col)
    odd_rows = -(becsum.T * parity_col)
    real_part = kind_onehot[:, None, :] * even_rows[None, :, :]
    imag_part = kind_onehot[:, None, :] * odd_rows[None, :, :]
    stacked = jnp.concatenate([real_part, imag_part], axis=2)
    return stacked.reshape(-1, stacked.shape[2]).astype(jnp.bfloat16)


def dense_augmentation(coefficients, atom_sites, column_x, column_y):
    slot_total = column_x.shape[0]
    zeros_z = jnp.zeros((1, NZ), jnp.int32)
    flat_x = (column_x[:, None] + zeros_z).reshape(-1)
    flat_y = (column_y[:, None] + zeros_z).reshape(-1)
    flat_z = (
        jnp.zeros((slot_total, 1), jnp.int32) + jnp.arange(NZ, dtype=jnp.int32)[None, :]
    ).reshape(-1)
    struct_re, struct_im = phase_angle(atom_sites, flat_x, flat_y, flat_z)
    atom_total = coefficients.shape[0] // 2
    amp_re = coefficients[:atom_total]
    amp_im = coefficients[atom_total:]
    aug_re = jnp.sum(amp_re * struct_re - amp_im * struct_im, axis=0)
    aug_im = jnp.sum(amp_re * struct_im + amp_im * struct_re, axis=0)
    return (aug_re.reshape(slot_total, NZ), aug_im.reshape(slot_total, NZ))


def inverse_tables(length):
    counter = jnp.arange(length, dtype=jnp.int32)
    turn_count = counter[:, None] * counter[None, :] % length
    angle_value = turn_count.astype(jnp.float32) * (2.0 * np.pi / length)
    return (jnp.cos(angle_value), jnp.sin(angle_value))


def inverse_transform(data_re, data_im, length):
    cosine_table, sine_table = inverse_tables(length)
    out_re = jnp.dot(data_re, cosine_table, precision=highest) - jnp.dot(
        data_im, sine_table, precision=highest
    )
    out_im = jnp.dot(data_re, sine_table, precision=highest) + jnp.dot(
        data_im, cosine_table, precision=highest
    )
    return (out_re, out_im)


def finish_planes(received):
    cosine_table, sine_table = inverse_tables(received.shape[2])
    out_re = jnp.einsum("pgy,gx->pyx", received[0], cosine_table, precision=highest) - jnp.einsum(
        "pgy,gx->pyx", received[1], sine_table, precision=highest
    )
    out_im = jnp.einsum("pgy,gx->pyx", received[0], sine_table, precision=highest) + jnp.einsum(
        "pgy,gx->pyx", received[1], cosine_table, precision=highest
    )
    return jnp.stack([out_re, out_im])


def on_device(
    waves, occupations, beta_table, wave_miller, atom_kinds, atom_sites, aug_table, stick_columns
):
    band_count = lax.axis_size("band")
    plane_groups = lax.axis_size("ga")
    band_dev = waves.shape[1]
    column_block = NX // band_count
    all_columns = lax.all_gather(stick_columns, "ga", axis=0, tiled=True)
    wave_matrix = jnp.concatenate(
        [
            jnp.concatenate([waves[0], waves[1]], axis=1),
            jnp.concatenate([waves[1], -waves[0]], axis=1),
        ],
        axis=0,
    )
    pair_index, factors, parity = pair_tables(NH)
    rows_here = ATOMS * NH // plane_groups
    atom_count = rows_here * lax.axis_size("ga") // NH
    atom_block = math.gcd(atom_count, 32)

    def project_block(block_index):
        start_atom = block_index * atom_block
        site_block = lax.dynamic_slice_in_dim(atom_sites, start_atom, atom_block, 1)
        kinds_block = lax.dynamic_slice_in_dim(atom_kinds, start_atom, atom_block, 0)
        vkb_re, vkb_im = projector_rows(site_block, kinds_block, beta_table, wave_miller)
        stacked = jnp.concatenate([vkb_re, vkb_im], axis=2).reshape(atom_block * NH, -1)
        return lax.dot_general(
            stacked, wave_matrix, (((1,), (1,)), ((), ())), preferred_element_type=jnp.float32
        )

    pieces = lax.map(project_block, jnp.arange(atom_count // atom_block, dtype=jnp.int32))
    becp_rows = lax.psum_scatter(
        pieces.reshape(rows_here * lax.axis_size("ga"), 2 * band_dev),
        "ga",
        scatter_dimension=0,
        tiled=True,
    )
    atom_count = becp_rows.shape[0] // NH
    blocks = becp_rows.reshape(atom_count, NH, 2 * band_dev)
    weights = jnp.concatenate([occupations, occupations])
    full_square = jnp.einsum(
        "aic,ajc->aij", blocks * weights[None, None, :], blocks, precision=highest
    )
    partial_value = full_square.reshape(atom_count, NH * NH)[:, pair_index] * factors[None, :]
    summed = lax.psum(partial_value, "band")
    becsum = lax.all_gather(summed, "ga", axis=0, tiled=True)
    aug_weights = augment_weights(becsum, atom_kinds)
    column_x = lax.axis_index("band") * column_block + stick_columns // NY
    column_y = stick_columns % NY
    coefficients = lax.dot_general(
        aug_weights, aug_table, (((0,), (0,)), ((), ())), preferred_element_type=jnp.float32
    )
    aug_re, aug_im = dense_augmentation(coefficients, atom_sites, column_x, column_y)
    stick_re, stick_im = inverse_transform(aug_re, aug_im, NZ)
    exchanged = lax.all_to_all(
        jnp.stack([stick_re, stick_im]), "ga", split_axis=2, concat_axis=1, tiled=True
    )
    plane_count = exchanged.shape[2]
    slot_rows = jnp.where(all_columns < 0, -1, all_columns)
    selector = (
        slot_rows[:, None] == jnp.arange(column_block * NY, dtype=jnp.int32)[None, :]
    ).astype(jnp.float32)
    planes = jnp.einsum("ctp,tr->cpr", exchanged, selector, precision=highest)
    planes = planes.reshape(2, plane_count, column_block, NY)
    plane_re, plane_im = inverse_transform(planes[0], planes[1], NY)
    density = finish_planes(
        lax.all_to_all(
            jnp.stack([plane_re, plane_im]), "band", split_axis=3, concat_axis=2, tiled=True
        )
    )
    return density


def solution(mesh):
    in_specs = (
        P(None, "band", "ga"),
        P("band"),
        P(None, "ga"),
        P(None, "ga"),
        P(),
        P(),
        P(None, ("band", "ga")),
        P(("band", "ga")),
    )
    out_specs = P(None, "ga", "band", None)
    return jax.shard_map(
        on_device, mesh=mesh, in_specs=in_specs, out_specs=out_specs, check_vma=False
    )
```

profile of v0, /device:TPU:0, one launch (start us, length us, event | category | flops | bytes accessed | tf_op | source)
XLA Modules:
  0.0 498.8 jit_solution(2643049800856077495)
XLA Ops:
  8.5 151.9 %while.14 = (s32[]{:T(128)}, f32[8,576,64]{1,2,0:T(8,128)}, s32[8]{0:T(128)S(1)}, s32[256]{0:T(256)}, f32[72,1024]{1,0:T(8,128)}, /*index=5*/s32[3,256]{1,0:T(4,...) while((s32[]{:T(128)}, f32[8,576,64]{1,2,0:T(8,128)}, ...), condition=%wide.region_1.2_spmd.clone, body=%wide.region_0.1_spmd.sunk.clone.sunk | while | flops 191037568 | bytes 20748900 | solution.py:149
  14.0 2.8 subtract_convert_fusion.2
  17.0 3.0 copy.78
  20.0 4.3 reshape.354
  24.3 3.1 fusion.199
  32.9 2.8 subtract_convert_fusion.2
  35.9 3.0 copy.78
  39.0 4.3 reshape.354
  43.3 3.1 fusion.199
  51.9 2.8 subtract_convert_fusion.2
  54.9 3.0 copy.78
  57.9 4.3 reshape.354
  62.3 3.1 fusion.199
  70.9 2.8 subtract_convert_fusion.2
  73.9 3.0 copy.78
  76.9 4.3 reshape.354
  81.3 3.1 fusion.199
  89.9 2.8 subtract_convert_fusion.2
  92.9 3.0 copy.78
  95.9 4.3 reshape.354
  100.2 3.1 fusion.199
  108.9 2.8 subtract_convert_fusion.2
  111.9 3.0 copy.78
  114.9 4.3 reshape.354
  119.2 3.2 fusion.199
  127.9 2.8 subtract_convert_fusion.2
  130.9 3.0 copy.78
  133.9 4.3 reshape.354
  138.2 3.1 fusion.199
  146.8 2.8 subtract_convert_fusion.2
  149.8 3.0 copy.78
  152.9 4.3 reshape.354
  157.2 3.1 fusion.199
  160.3 2.9 copy.69
  167.0 10.0 %all-reduce = s32[64]{0:T(128)} all-reduce(s32[64]{0:T(128)S(1)} %dynamic-update-slice), channel_id=1, replica_groups=mesh['band'=4,'ga'=8] {'ga'}, use_global_device_ids=true, to_apply=%add | all-reduce | flops 64 | bytes 512
  178.3 30.1 %reduce-scatter.4.cloned.1.call-done = f32[576,64]{1,0:T(8,128)} async-done(((f32[4608,64]{1,0:T(8,128)}), f32[576,64]{1,0:T(8,128)}) %reduce-scatter.4.cloned.1.call-update) | async-done | bytes 147472 | tf_op jit(solution)/shard_map/reduce_scatter | solution.py:150
  211.3 20.5 %psum.7 = f32[32,171]{0,1:T(8,128)S(1)} all-reduce(f32[32,171]{0,1:T(8,128)S(1)} %multiply_bitcast_fusion.1), channel_id=1, replica_groups=mesh['band'=4,'ga'=8] {'band'}, use_global_device_ids=true, to_apply=%region_3.4 | all-reduce | flops 5472 | bytes 43776 | tf_op jit(solution)/shard_map/psum | solution.py:163
  231.9 9.8 %all_gather.6 = f32[256,171]{1,0:T(8,128)S(1)} all-gather(f32[32,171]{1,0:T(8,128)S(1)} %copy.53), channel_id=1, replica_groups=mesh['band'=4,'ga'=8] {'ga'}, dimensions={0}, use_global_device_ids=true | all-gather | bytes 196992 | tf_op jit(solution)/shard_map/all_gather | solution.py:164
  244.7 11.8 %add_reduce_fusion = (f32[1792]{0:T(1024)S(1)}, f32[1792]{0:T(1024)S(1)}) fusion(f32[512,1792]{1,0:T(8,128)S(1)} %fusion.46, s32[1792]{0:T(1024)S(1)} %copy-done.6, s32[256]{0:T(256)S(1)} %bitcast.130, s32[1792]{0:T(1024)S(1)} %copy-done.5, s32[256]{0:T(256)S(1)} %bitcast.131, s32[1792]{0:T(1024)S(1)} %mul.522, s32[256]{0:T(256)S(1)} %bitcast.129), kind=kLoop, calls=%fused_computation.61 | loop fusion | flops 19264000 | bytes 3708928 | tf_op jit(solution)/shard_map/reduce_sum | solution.py:86
  262.3 3.5 all-to-all-start
  265.8 4.6 all-to-all-done
  276.3 3.1 squeeze.33
  279.4 3.8 fusion.57
  283.3 3.8 fusion.64
  287.0 3.4 squeeze.34
  290.4 4.3 subtract_bitcast_fusion.1
  294.7 2.7 add_bitcast_fusion.1
  297.4 2.1 pad_maximum_fusion.1
  299.6 10.1 %copy.59 = f32[2,28,60,240]{2,0,1,3:T(2,128)} copy(f32[2,28,60,240]{3,2,1,0:T(8,128)} %pad_maximum_fusion.1) | data formatting | bytes 6451200 | tf_op jit(solution)/shard_map/stack | solution.py:186
  309.7 17.1 %reshape.349 = f32[4,1,201600]{2,1,0:T(1,128)} reshape(f32[240,28,2,60]{3,2,1,0:T(2,128)} %bitcast.121) | data formatting | bytes 6451200
  326.8 78.3 %all_to_all.33 = f32[4,1,201600]{2,1,0:T(1,128)} all-to-all(f32[4,1,201600]{2,1,0:T(1,128)} %reshape.349), channel_id=1, replica_groups=mesh['band'=4,'ga'=8] {'band'}, dimensions={0} | all-to-all | bytes 6451200 | tf_op jit(solution)/shard_map/all_to_all | solution.py:185
  405.1 11.9 %reduce.1 = f32[4,201600]{1,0:T(4,128)} reduce(f32[4,1,201600]{2,1,0:T(1,128)} %all_to_all.33, f32[]{:T(128)} %broadcast.506), dimensions={1}, to_apply=%all_to_all.28.reduce_sub_computation | reduce | bytes 6451204 | tf_op jit(solution)/shard_map/all_to_all | solution.py:185
  417.0 18.0 %reshape.350 = f32[240,28,2,60]{3,2,1,0:T(2,128)} reshape(f32[4,201600]{1,0:T(4,128)} %reduce.1) | data formatting | bytes 6451200
  435.0 12.1 %copy.66 = f32[2,28,60,4,60]{4,3,0,2,1:T(4,128)} copy(f32[2,28,60,4,60]{2,0,1,4,3:T(2,128)} %bitcast.122) | data formatting | bytes 6451200 | tf_op jit(solution)/shard_map/all_to_all | solution.py:185
  447.1 6.4 %fusion.171 = (f32[1,28,4,60,60]{4,2,0,3,1:T(4,128)}, f32[1,28,4,60,60]{4,2,0,3,1:T(4,128)}) fusion(f32[2,28,4,60,60]{4,2,0,3,1:T(4,128)} %bitcast.120), kind=kLoop, calls=%fused_computation.201 | loop fusion | bytes 6451200 | tf_op jit(solution)/shard_map/slice | solution.py:111
  453.5 5.9 %copy.61 = f32[1,28,4,60,60]{3,2,4,1,0:T(4,128)} copy(f32[1,28,4,60,60]{4,2,0,3,1:T(4,128)} %get-tuple-element.225) | data formatting | bytes 3225600 | tf_op jit(solution)/shard_map/slice | solution.py:110
  459.3 3.5 squeeze.35
  462.9 3.8 fusion.54
  466.7 3.8 fusion.61
  470.5 5.9 %copy.62 = f32[1,28,4,60,60]{3,2,4,1,0:T(4,128)} copy(f32[1,28,4,60,60]{4,2,0,3,1:T(4,128)} %get-tuple-element.224) | data formatting | bytes 3225600 | tf_op jit(solution)/shard_map/slice | solution.py:111
  476.4 3.6 squeeze.36
  480.0 4.3 subtract_bitcast_fusion
  484.3 2.7 add_bitcast_fusion
  487.3 4.4 copy.63
  (154 shorter events, 64.1 us)
Async XLA Ops:
  6.5 236.4 %copy-start = (bf16[684,1792]{1,0:T(8,128)(2,1)S(1)}, bf16[684,1792]{1,0:T(8,128)(2,1)}, u32[]{:S(2)}) copy-start(bf16[684,1792]{1,0:T(8,128)(2,1)} %param.22) | copy-start | bytes 7354372
  6.5 202.0 %reduce-scatter.4.cloned.1.call-start = ((), (), s32[]{:S(2)}) async-start(), calls=%async_computation.3 | async-start | bytes 2654208 | tf_op jit(solution)/shard_map/reduce_scatter | solution.py:150
  163.2 0.7 copy-start.15
  163.2 2.2 copy-start.17
  163.2 13.9 %copy-start.16 = (f32[32]{0:T(128)S(1)}, f32[32]{0:T(128)}, u32[]{:S(2)}) copy-start(f32[32]{0:T(128)} %param.17) | copy-start | bytes 388
  163.2 13.9 %copy-start.14 = (s32[171]{0:T(256)S(1)}, s32[171]{0:T(256)}, u32[]{:S(2)}) copy-start(s32[171]{0:T(256)} %constant.199) | copy-start | bytes 2056
  163.2 13.9 %copy-start.13 = (s32[256]{0:T(256)S(1)}, s32[256]{0:T(256)}, u32[]{:S(2)}) copy-start(s32[256]{0:T(256)} %get-tuple-element.356) | copy-start | bytes 3076
  163.2 14.5 %copy-start.4 = (s32[3,256]{1,0:T(4,128)S(1)}, s32[3,256]{1,0:T(4,128)}, u32[]{:S(2)}) copy-start(s32[3,256]{1,0:T(4,128)} %get-tuple-element.355) | copy-start | bytes 9220
  163.3 48.0 %copy-start.12 = (f32[171]{0:T(256)S(1)}, f32[171]{0:T(256)}, u32[]{:S(2)}) copy-start(f32[171]{0:T(256)} %constant.196) | copy-start | bytes 2056
  164.1 77.6 %copy-start.10 = (f32[171]{0:T(256)S(1)}, f32[171]{0:T(256)}, u32[]{:S(2)}) copy-start(f32[171]{0:T(256)} %constant.198) | copy-start | bytes 2056
  164.1 77.6 %copy-start.11 = (f32[171]{0:T(256)S(1)}, f32[171]{0:T(256)}, u32[]{:S(2)}) copy-start(f32[171]{0:T(256)} %constant.193.clone) | copy-start | bytes 2056
  243.0 1.7 copy-start.5
  243.0 1.7 copy-start.6
  243.0 1.7 copy-start.7
  243.0 1.7 copy-start.8
  243.0 1.7 copy-start.9
  256.6 9.2 %copy-start.18 = (s32[64]{0:T(128)S(1)}, s32[64]{0:T(128)}, u32[]{:S(2)}) copy-start(s32[64]{0:T(128)} %all-reduce) | copy-start | bytes 772
  262.3 8.2 %all-to-all-start = ((f32[8,1,448]{2,1,0:T(1,128)}), f32[8,1,448]{2,1,0:T(1,128)S(1)}, u32[]{:S(2)}, u32[]{:S(2)}) async-start(f32[8,1,448]{2,1,0:T(1,128)} %reshape.347), calls=%async_computation | async-start | bytes 32768 | tf_op jit(solution)/shard_map/all_to_all | solution.py:173
  290.4 4.3 copy-start.3
  479.9 4.3 copy-start.2
  487.0 4.7 copy-start.1
Sparse Core Ops, SparseCore 0:
  163.4 45.0 reduce-scatter.3
where the time goes:
time: 508 us; the launch traced here: 499 us
  local copies, waits for them, and re-layouts  198 us (39%)
  blocking collectives  119 us (23%)
  matrix products  85.2 us (17%)
  other arithmetic  38.3 us (8%)
  waiting for transfers between devices  34.8 us (7%)
  between operations  14.8 us (3%)
  loops' own time  5.5 us (1%)
    all_to_all x1, blocking collectives, on_device(): lax.all_to_all(jnp.stack([plane_re, plane_im]), 'band', split_axis=3, con...  78.3 us
    unnamed x46, local copies, waits for them, and re-layouts  40.8 us
    reshape x8, local copies, waits for them, and re-layouts, project_block(): jnp.concatenate([vkb_re, vkb_im], axis=2).reshape(atom_block * NH, -1)  34.6 us
    reduce_scatter x1, waiting for transfers between devices, on_device(): lax.psum_scatter(pieces.reshape(rows_here * lax.axis_size('ga'), 2 * band...  30.1 us
    dot_general x8, matrix products, project_block(): lax.dot_general(stacked, wave_matrix, (((1,), (1,)), ((), ())), preferred...  25.1 us
    concatenate x8, local copies, waits for them, and re-layouts, project_block(): jnp.concatenate([vkb_re, vkb_im], axis=2).reshape(atom_block * NH, -1)  24.3 us
    dot_general x8, matrix products, projector_rows(): jnp.einsum('as,sig->aig', kind_onehot, table_three, precision=highest)  22.1 us
    psum x1, blocking collectives, on_device(): summed = lax.psum(partial_value, 'band')  20.5 us
  transfers between devices with their start and end apart: 2, of which 2 were waited for; matrix products, arithmetic and copies ran while one was open for 1% of the time, Pallas kernels for 0%

commit v1 on v0

v1 whole, which is shorter than its diff:
```python
import functools
import math

import jax
import jax.numpy as jnp
import numpy as np
from jax import lax
from jax.experimental import pallas as pl
from jax.experimental.pallas import tpu as pltpu
from jax.sharding import PartitionSpec as P

NX = 240
NY = 240
NZ = 224
NH = 18
HALF = NH // 2
SPECIES = 4

PERIOD = math.lcm(NX, NY, NZ)
STEP_X = PERIOD // NX
STEP_Y = PERIOD // NY
STEP_Z = PERIOD // NZ
ELL = np.array([0, 0] + [1] * 6 + [2] * 10)
PAIR_FIRST, PAIR_SECOND = np.triu_indices(NH)

highest = lax.Precision.HIGHEST
F32 = jnp.float32
BF16 = jnp.bfloat16


def fit_even(func, terms):
    nodes = 0.125 * (1.0 + np.cos(np.pi * (np.arange(64) + 0.5) / 64))
    scaled = np.polynomial.chebyshev.Chebyshev.fit(nodes, func(np.sqrt(nodes)), terms - 1, domain=[0, 0.25])
    return [float(c) for c in scaled.convert(kind=np.polynomial.Polynomial).coef]


COS_FIT = fit_even(lambda u: np.cos(2 * np.pi * u), 7)
SIN_FIT = fit_even(lambda u: np.sin(2 * np.pi * u) / u, 6)


def horner(coefs, w):
    total = jnp.full_like(w, coefs[-1])
    for c in coefs[-2::-1]:
        total = total * w + c
    return total


def turn_cos_sin(count, period):
    rest = count - jnp.round(count * (1.0 / period)) * period
    u = rest * (1.0 / period)
    w = u * u
    return horner(COS_FIT, w), u * horner(SIN_FIT, w)


def projection_kernel(sites_ref, kinds_ref, miller_ref, beta_ref, wave_ref, out_ref, rows_ref):
    block = sites_ref.shape[0]
    width = miller_ref.shape[1]
    site = sites_ref[...]
    miller = miller_ref[...]
    count = site[:, 0:1] * miller[0:1, :] + site[:, 1:2] * miller[1:2, :] + site[:, 2:3] * miller[2:3, :]
    cosine, sine = turn_cos_sin(count, PERIOD)
    kinds = kinds_ref[...]
    masks = [kinds == s for s in range(1, SPECIES)]
    for i in range(NH):
        radial = jnp.broadcast_to(beta_ref[i : i + 1, :], (block, width))
        for s in range(1, SPECIES):
            radial = jnp.where(masks[s - 1], beta_ref[s * NH + i : s * NH + i + 1, :], radial)
        if ELL[i] == 0:
            real, imag = radial * cosine, -(radial * sine)
        elif ELL[i] == 1:
            real, imag = -(radial * sine), -(radial * cosine)
        else:
            real, imag = -(radial * cosine), radial * sine
        row = (i % HALF) * block
        col = (i // HALF) * 2 * width
        rows_ref[row : row + block, col : col + width] = real.astype(BF16)
        rows_ref[row : row + block, col + width : col + 2 * width] = imag.astype(BF16)
    result = jnp.dot(rows_ref[...], wave_ref[...], preferred_element_type=F32)
    out_ref[...] = result.reshape(HALF, block, result.shape[1])


def project(sites, kinds, miller, beta_table, wave_matrix):
    atoms = sites.shape[0]
    width = miller.shape[1]
    cols = wave_matrix.shape[1]
    block = math.gcd(atoms, 32)
    whole = lambda a: pl.BlockSpec(a.shape, lambda b: (0, 0))
    return pl.pallas_call(
        projection_kernel,
        grid=(atoms // block,),
        in_specs=[
            pl.BlockSpec((block, 3), lambda b: (b, 0)),
            pl.BlockSpec((block, 1), lambda b: (b, 0)),
            whole(miller),
            whole(beta_table),
            whole(wave_matrix),
        ],
        out_specs=pl.BlockSpec((HALF, block, cols), lambda b: (0, b, 0)),
        out_shape=jax.ShapeDtypeStruct((HALF, atoms, cols), F32),
        scratch_shapes=[pltpu.VMEM((HALF * block, 4 * width), BF16)],
        name="project",
    )(sites, kinds, miller, beta_table, wave_matrix)


def dense_kernel(weights_ref, table_ref, sites_ref, points_ref, out_ref):
    atoms = sites_ref.shape[0]
    coef = jnp.dot(weights_ref[...], table_ref[...], preferred_element_type=F32)
    site = sites_ref[...]
    points = points_ref[...]
    count = site[:, 0:1] * points[0:1, :] + site[:, 1:2] * points[1:2, :] + site[:, 2:3] * points[2:3, :]
    cosine, sine = turn_cos_sin(count, PERIOD)
    real, imag = coef[:atoms], coef[atoms:]
    out_ref[0:1, :] = jnp.sum(real * cosine + imag * sine, axis=0, keepdims=True)
    out_ref[1:2, :] = jnp.sum(imag * cosine - real * sine, axis=0, keepdims=True)


def dense(weights, table, sites, points):
    rows, cols = table.shape
    tile = math.gcd(cols, 256)
    return pl.pallas_call(
        dense_kernel,
        grid=(cols // tile,),
        in_specs=[
            pl.BlockSpec(weights.shape, lambda c: (0, 0)),
            pl.BlockSpec((rows, tile), lambda c: (0, c)),
            pl.BlockSpec(sites.shape, lambda c: (0, 0)),
            pl.BlockSpec((3, tile), lambda c: (0, c)),
        ],
        out_specs=pl.BlockSpec((2, tile), lambda c: (0, c)),
        out_shape=jax.ShapeDtypeStruct((2, cols), F32),
        name="dense",
    )(weights, table, sites, points)


def augment_weights(becsum, atom_kinds):
    odd = jnp.asarray((ELL[PAIR_FIRST] + ELL[PAIR_SECOND]) % 2 == 1)[None, :]
    even_rows = jnp.where(odd, 0.0, becsum)
    odd_rows = jnp.where(odd, -becsum, 0.0)
    stacked = jnp.concatenate([even_rows, odd_rows], axis=0).astype(BF16)
    kinds = jnp.concatenate([atom_kinds, atom_kinds])[:, None]
    parts = [jnp.where(kinds == s, stacked, jnp.zeros_like(stacked)) for s in range(SPECIES)]
    return jnp.concatenate(parts, axis=1)


def table_of(rows, cols, period):
    angle = (np.outer(rows, cols) % period) * (2.0 * np.pi / period)
    return np.cos(angle).astype(np.float32), np.sin(angle).astype(np.float32)


def on_device(
    waves, occupations, beta_table, wave_miller, atom_kinds, atom_sites, aug_table, stick_columns
):
    bands = lax.axis_size("band")
    groups = lax.axis_size("ga")
    atoms = atom_sites.shape[1]
    slots = stick_columns.shape[0]
    column_block = NX // bands
    y_block = NY // bands
    planes = NZ // groups
    steps = jnp.asarray([STEP_X, STEP_Y, STEP_Z], F32)
    sites = atom_sites.T.astype(F32) * steps[None, :]

    wave_t = jnp.concatenate(
        [
            jnp.concatenate([waves[0], waves[1]], axis=1),
            jnp.concatenate([waves[1], -waves[0]], axis=1),
        ],
        axis=0,
    ).T
    empty = jnp.zeros_like(wave_t)
    wave_matrix = jnp.concatenate(
        [jnp.concatenate([wave_t, empty], axis=1), jnp.concatenate([empty, wave_t], axis=1)], axis=0
    )
    pieces = project(sites, atom_kinds[:, None], wave_miller.astype(F32), beta_table, wave_matrix)
    own = lax.psum_scatter(pieces, "ga", scatter_dimension=1, tiled=True)
    own_atoms = own.shape[1]
    blocks = own.reshape(HALF, own_atoms, 2, wave_t.shape[1]).transpose(1, 2, 0, 3)
    blocks = blocks.reshape(own_atoms, NH, wave_t.shape[1])
    occupied = jnp.concatenate([occupations, occupations])
    square = jnp.einsum("aic,ajc->aij", blocks * occupied[None, None, :], blocks, precision=highest)
    factors = np.where(PAIR_FIRST == PAIR_SECOND, 1.0, 2.0).astype(np.float32)
    partial_value = square.reshape(own_atoms, NH * NH)[:, PAIR_FIRST * NH + PAIR_SECOND] * factors[None, :]
    becsum = lax.all_gather(lax.psum(partial_value, "band"), "ga", axis=0, tiled=True)
    weights = augment_weights(becsum, atom_kinds)

    column_x = lax.axis_index("band") * column_block + stick_columns // NY
    column_y = stick_columns % NY
    ones_z = jnp.ones((1, NZ), jnp.int32)
    points = jnp.stack(
        [
            (column_x[:, None] * ones_z).reshape(-1),
            (column_y[:, None] * ones_z).reshape(-1),
            (jnp.arange(NZ, dtype=jnp.int32)[None, :] + jnp.zeros((slots, 1), jnp.int32)).reshape(-1),
        ]
    ).astype(F32)
    aug = dense(weights, aug_table, sites, points).reshape(2, slots, NZ)
    cos_z, sin_z = table_of(np.arange(NZ), np.arange(NZ), NZ)
    both = jnp.dot(aug.reshape(2 * slots, NZ), np.concatenate([cos_z, sin_z], axis=1), precision=highest)
    both = both.reshape(2, slots, 2, NZ)
    stick_re = both[0, :, 0] - both[1, :, 1]
    stick_im = both[0, :, 1] + both[1, :, 0]
    packed = jnp.concatenate(
        [
            stick_re.reshape(slots, groups, planes),
            stick_im.reshape(slots, groups, planes),
            jnp.broadcast_to(stick_columns.astype(F32)[:, None, None], (slots, groups, 1)),
        ],
        axis=2,
    ).transpose(1, 0, 2)
    received = lax.all_to_all(packed, "ga", split_axis=0, concat_axis=0, tiled=True)
    received = lax.all_gather(received.reshape(groups * slots, -1), "band", axis=0, tiled=True)
    return finish(received, planes, y_block, column_block, groups * slots)


def finish(received, planes, y_block, column_block, block_sticks):
    total = received.shape[0]
    columns = received[:, 2 * planes]
    live = columns >= 0
    value_re = jnp.where(live[:, None], received[:, :planes], 0.0)
    value_im = jnp.where(live[:, None], received[:, planes : 2 * planes], 0.0)
    columns = columns.astype(jnp.int32)
    gx = ((jnp.arange(total, dtype=jnp.int32) // block_sticks) * column_block + columns // NY).astype(F32)
    gy = (columns % NY).astype(F32)
    y_values = (lax.axis_index("band") * y_block + jnp.arange(y_block, dtype=jnp.int32)).astype(F32)
    cos_y, sin_y = turn_cos_sin(gy[:, None] * y_values[None, :], NY)
    cos_x, sin_x = turn_cos_sin(gx[:, None] * jnp.arange(NX, dtype=jnp.int32).astype(F32)[None, :], NX)
    amp_re = value_re[:, :, None] * cos_y[:, None, :] - value_im[:, :, None] * sin_y[:, None, :]
    amp_im = value_re[:, :, None] * sin_y[:, None, :] + value_im[:, :, None] * cos_y[:, None, :]
    amp = jnp.concatenate([amp_re, amp_im], axis=0)
    dims = (((0,), (0,)), ((), ()))
    wave_re = jnp.concatenate([cos_x, -sin_x], axis=0)
    wave_im = jnp.concatenate([sin_x, cos_x], axis=0)
    out_re = lax.dot_general(amp, wave_re, dims, precision=lax.Precision.HIGH)
    out_im = lax.dot_general(amp, wave_im, dims, precision=lax.Precision.HIGH)
    return jnp.stack([out_re, out_im])


def solution(mesh):
    in_specs = (
        P(None, "band", "ga"),
        P("band"),
        P(None, "ga"),
        P(None, "ga"),
        P(),
        P(),
        P(None, ("band", "ga")),
        P(("band", "ga")),
    )
    out_specs = P(None, "ga", "band", None)
    return jax.shard_map(
        on_device, mesh=mesh, in_specs=in_specs, out_specs=out_specs, check_vma=False
    )
```

time: 508 us -> 150 us (0.30); the launches traced: 499 us -> 150 us
  local copies, waits for them, and re-layouts: 198 us -> 13.2 us
  matrix products: 85.2 us -> 4.89 us
  blocking collectives: 119 us -> 42 us
  other arithmetic: 38.3 us -> 10.2 us
  Pallas kernels: 0 us -> 19.3 us
  waiting for transfers between devices: 34.8 us -> 43 us
  loops' own time: 5.5 us -> 0 us
    dot_general x31 -> x4, matrix products: 85.2 us -> 4.89 us  [the longest x1 1.68 us: finish(): out_re = lax.dot_general(amp, wave_re, dims, precision=lax.Precision.HIGH)]
    all_to_all x1 -> x0, blocking collectives: 78.3 us -> none  [on_device(): lax.all_to_all(jnp.stack([plane_re, plane_im]), 'band', split_axis=3, con...]
    reshape x21 -> x4, local copies, waits for them, and re-layouts: 44 us -> 1.38 us  [the longest x2 1.13 us: on_device(): own.reshape(HALF, own_atoms, 2, wave_t.shape[1]).transpose(1, 2, 0, 3)]
    unnamed x46 -> x17, local copies, waits for them, and re-layouts: 40.8 us -> 0.83 us
    slice x13 -> x0, local copies, waits for them, and re-layouts: 27.6 us -> none  [the longest x2 12.3 us: finish_planes(): received[1]]
    concatenate x8 -> x4, local copies, waits for them, and re-layouts: 24.3 us -> 2.03 us  [the longest x2 1.48 us: augment_weights(): kinds = jnp.concatenate([atom_kinds, atom_kinds])[:, None]]
    pallas_call x0 -> x2, Pallas kernels: none -> 19.3 us  [the longest x1 12 us: project(): pl.pallas_call(projection_kernel, grid=(atoms // block,), in_specs=[pl.Bl...]
    dynamic_slice x24 -> x0, local copies, waits for them, and re-layouts: 16.7 us -> none  [the longest x8 6.05 us: project_block(): lax.dynamic_slice_in_dim(atom_kinds, start_atom, atom_block, 0)]
where the time goes in v1:
time: 150 us
  waiting for transfers between devices  43 us (29%)
  blocking collectives  42 us (28%)
  Pallas kernels  19.3 us (13%)
  between operations  13.7 us (9%)
  local copies, waits for them, and re-layouts  13.2 us (9%)
  other arithmetic  10.2 us (7%)
  matrix products  4.89 us (3%)
  starting transfers between devices  3.34 us (2%)
    reduce_scatter x1, waiting for transfers between devices, on_device(): own = lax.psum_scatter(pieces, 'ga', scatter_dimension=1, tiled=True)  38.3 us
    psum x1, blocking collectives, on_device(): lax.psum(partial_value, 'band')  19 us
    all_gather x1, blocking collectives, on_device(): lax.all_gather(received.reshape(groups * slots, -1), 'band', axis=0, tile...  13.7 us
    pallas_call x1, Pallas kernels, project(): pl.pallas_call(projection_kernel, grid=(atoms // block,), in_specs=[pl.Bl...  12 us
    all_gather x1, blocking collectives, on_device(): lax.all_gather(lax.psum(partial_value, 'band'), 'ga', axis=0, tiled=True)  9.26 us
    pallas_call x1, Pallas kernels, dense(): pl.pallas_call(dense_kernel, grid=(cols // tile,), in_specs=[pl.BlockSpec...  7.29 us
    all_to_all x1, waiting for transfers between devices, on_device(): lax.all_to_all(packed, 'ga', split_axis=0, concat_axis=0, tiled=True)  4.67 us
    another operation x1, local copies, waits for them, and re-layouts, finish(): return jnp.stack([out_re, out_im])  4.42 us
  transfers between devices with their start and end apart: 2, of which 2 were waited for; matrix products, arithmetic and copies ran while one was open for 1% of the time, Pallas kernels for 0%

profile of v1, /device:TPU:0, one launch (start us, length us, event | category | flops | bytes accessed | tf_op | source)
XLA Modules:
  0.0 149.6 jit_solution(2403234830657149301)
XLA Ops:
  6.5 0.0 reduce-scatter.2.cloned.1.call-start
  6.5 0.8 fusion.85
  7.4 0.9 slice_bitcast_fusion.1
  8.3 1.3 convert_element_type.42.miller_ref
  9.6 0.8 convert_multiply_fusion
  10.3 0.8 copy.68
  11.1 1.5 copy.71.kinds_ref
  12.6 0.3 copy.69
  12.9 0.3 copy.70
  13.2 0.3 maximum_bitcast_fusion
  13.5 1.3 fusion.6.wave_ref
  14.8 12.0 %project.1 = f32[9,256,128]{2,1,0:T(8,128)} custom-call(f32[256,3]{1,0:T(8,128)} %bitcast.43, s32[256,1]{1,0:T(8,128)} %copy.71.kinds_ref, f32[3,1024]{1,0:T(4,128)} %convert_element_type.42.miller_ref, f32[72,1024]{1,0:T(8,128)} %beta_ref.1, bf16[4096,128]{1,0:T(8,128)(2,1)} %fusion.6.wave_ref), custom_call_target="tpu_custom_call" | custom-call | tf_op jit(solution)/shard_map/project/pallas_call | solution.py:88
  26.8 0.0 reduce-scatter.2.cloned.1.call-update
  26.8 0.0 copy-done.5
  26.8 0.1 mul.303
  26.9 0.1 stack_reshape.9
  27.0 0.1 mul.304
  27.1 0.1 stack_reshape.10
  27.2 0.1 stack_reshape.11
  27.2 0.0 copy-done.6
  27.3 0.1 pad_maximum_fusion.12
  27.3 0.0 copy-done.1
  27.4 0.0 copy-done.4
  27.4 0.6 add_convert_fusion.points_ref
  28.0 38.3 %reduce-scatter.2.cloned.1.call-done = f32[9,32,128]{2,1,0:T(8,128)} async-done(((f32[9,256,128]{2,1,0:T(8,128)}), f32[9,32,128]{2,1,0:T(8,128)}) %reduce-scatter.2.cloned.1.call-update) | async-done | bytes 147472 | tf_op jit(solution)/shard_map/reduce_scatter | solution.py:175
  66.3 1.1 reshape.220
  67.5 0.0 copy-start.2
  67.5 1.1 fusion.11
  68.6 0.1 reshape.236
  68.8 0.1 copy.83
  68.9 0.7 gather_fusion
  69.6 0.1 copy.76
  69.6 0.0 copy-done.3
  69.7 19.0 %psum.7 = f32[32,171]{1,0:T(8,128)S(1)} all-reduce(f32[32,171]{1,0:T(8,128)S(1)} %multiply_bitcast_fusion), channel_id=1, replica_groups=mesh['band'=4,'ga'=8] {'band'}, use_global_device_ids=true, to_apply=%region_1.0 | all-reduce | flops 5472 | bytes 43776 | tf_op jit(solution)/shard_map/psum | solution.py:183
  88.7 9.3 %all_gather.6 = f32[256,171]{1,0:T(8,128)S(1)} all-gather(f32[32,171]{1,0:T(8,128)S(1)} %psum.7), channel_id=1, replica_groups=mesh['band'=4,'ga'=8] {'ga'}, dimensions={0}, use_global_device_ids=true | all-gather | bytes 196992 | tf_op jit(solution)/shard_map/all_gather | solution.py:183
  97.9 0.0 copy-done.2
  98.0 0.9 broadcast_select_fusion.3
  98.9 1.3 pad_maximum_fusion.8.weights_ref
  100.2 7.3 %dense.1 = f32[2,1792]{1,0:T(2,128)} custom-call(bf16[512,684]{1,0:T(8,128)(2,1)} %pad_maximum_fusion.8.weights_ref, bf16[684,1792]{1,0:T(8,128)(2,1)} %table_ref.1, f32[256,3]{1,0:T(8,128)} %bitcast.44, f32[3,1792]{1,0:T(4,128)} %add_convert_fusion.points_ref), custom_call_target="tpu_custom_call" | custom-call | tf_op jit(solution)/shard_map/dense/pallas_call | solution.py:120
  107.5 0.8 reshape.232
  108.3 0.4 fusion.80
  108.7 0.1 sub.39
  108.8 0.1 add.256
  108.9 0.1 broadcast_in_dim.112
  109.0 0.1 maximum_bitcast_fusion.5
  109.1 0.7 reshape.241
  109.8 3.3 %all-to-all-start = ((f32[8,1,456]{2,1,0:T(1,128)}), f32[8,1,456]{2,1,0:T(1,128)S(1)}, u32[]{:S(2)}, u32[]{:S(2)}) async-start(f32[8,1,456]{2,1,0:T(1,128)} %reshape.241), calls=%async_computation.1 | async-start | bytes 32768 | tf_op jit(solution)/shard_map/all_to_all | solution.py:210
  113.2 4.7 %all-to-all-done = f32[8,1,456]{2,1,0:T(1,128)S(1)} async-done(((f32[8,1,456]{2,1,0:T(1,128)}), f32[8,1,456]{2,1,0:T(1,128)S(1)}, u32[]{:S(2)}, u32[]{:S(2)}) %all-to-all-start) | async-done | bytes 14624 | tf_op jit(solution)/shard_map/all_to_all | solution.py:210
  117.8 0.5 broadcast.255
  118.3 0.7 reduce.6
  119.0 0.1 reshape.242
  119.1 13.7 %all_gather.7 = f32[256,57]{1,0:T(8,128)S(1)} all-gather(f32[64,57]{1,0:T(8,128)S(1)} %bitcast.45), channel_id=1, replica_groups=mesh['band'=4,'ga'=8] {'band'}, dimensions={0}, use_global_device_ids=true | all-gather | bytes 72960 | tf_op jit(solution)/shard_map/all_gather | solution.py:211
  132.8 0.2 compare_reduce_fusion
  133.0 0.3 fusion.46
  133.3 0.1 slice_select_fusion.1
  133.5 0.1 copy.79
  133.6 0.1 copy.80
  133.7 0.2 fusion.74
  133.8 0.3 fusion.52
  134.1 0.5 multiply_subtract_fusion
  134.7 1.7 %fusion.5 = f32[1,28,60,240]{3,2,1,0:T(8,128)S(1)} fusion(f32[256,28,60]{0,2,1:T(8,128)S(1)} %get-tuple-element.12, f32[256,28,60]{0,2,1:T(8,128)S(1)} %get-tuple-element.11, f32[256,240]{0,1:T(8,128)S(1)} %get-tuple-element.23, f32[256,240]{0,1:T(8,128)S(1)} %get-tuple-element.22), kind=kOutput, calls=%fused_computation.12 | convolution fusion | flops 1239613440 | bytes 5544960 | tf_op jit(solution)/shard_map/dot_general | solution.py:234
  136.4 1.7 %fusion.4 = f32[1,28,60,240]{3,2,1,0:T(8,128)S(1)} fusion(f32[256,28,60]{0,2,1:T(8,128)S(1)} %get-tuple-element.12, f32[256,28,60]{0,2,1:T(8,128)S(1)} %get-tuple-element.11, f32[256,240]{0,1:T(8,128)S(1)} %get-tuple-element.21, f32[256,240]{0,1:T(8,128)S(1)} %get-tuple-element.23), kind=kOutput, calls=%fused_computation.11 | convolution fusion | flops 1239613440 | bytes 5544960 | tf_op jit(solution)/shard_map/dot_general | solution.py:233
  138.0 0.3 pad_maximum_fusion.1
  138.3 4.4 %copy.81 = f32[2,28,60,240]{3,0,2,1:T(2,128)} copy(f32[2,28,60,240]{3,2,1,0:T(8,128)S(1)} %pad_maximum_fusion.1) | data formatting | bytes 6451200 | tf_op jit(solution)/shard_map/stack | solution.py:235
  (25 shorter events, 0.3 us)
Async XLA Ops:
  6.5 59.8 %reduce-scatter.2.cloned.1.call-start = ((), (), s32[]{:S(2)}) async-start(), calls=%async_computation.2 | async-start | bytes 1327104 | tf_op jit(solution)/shard_map/reduce_scatter | solution.py:175
  14.7 12.1 %copy-start.5 = (s32[8]{0:T(128)S(1)}, s32[8]{0:T(128)}, u32[]{:S(2)}) copy-start(s32[8]{0:T(128)} %param.21) | copy-start | bytes 100
  14.7 12.5 %copy-start.6 = (f32[32]{0:T(128)S(1)}, f32[32]{0:T(128)}, u32[]{:S(2)}) copy-start(f32[32]{0:T(128)} %param.15) | copy-start | bytes 388
  14.7 12.6 %copy-start.1 = (s32[256]{0:T(256)S(1)}, s32[256]{0:T(256)}, u32[]{:S(2)}) copy-start(s32[256]{0:T(256)} %param.18) | copy-start | bytes 3076
  14.7 12.6 %copy-start.4 = (s32[171]{0:T(256)S(1)}, s32[171]{0:T(256)}, u32[]{:S(2)}) copy-start(s32[171]{0:T(256)} %constant.138) | copy-start | bytes 2056
  28.0 41.6 %copy-start.3 = (f32[171]{0:T(256)S(1)}, f32[171]{0:T(256)}, u32[]{:S(2)}) copy-start(f32[171]{0:T(256)} %constant.135) | copy-start | bytes 2056
  67.5 30.5 %copy-start.2 = (pred[171]{0:T(512)(128)(4,1)S(1)}, pred[171]{0:T(512)(128)(4,1)}, u32[]{:S(2)}) copy-start(pred[171]{0:T(512)(128)(4,1)} %constant.127.clone) | copy-start | bytes 517
  100.2 8.1 %copy-start = (f32[2,224,224,1]{2,1,0,3:T(8,128)S(1)}, f32[2,224,224,1]{2,1,0,3:T(8,128)}, u32[]{:S(2)}) copy-start(f32[2,224,224,1]{2,1,0,3:T(8,128)} %constant.139) | copy-start | bytes 1204228
  109.8 8.0 %all-to-all-start = ((f32[8,1,456]{2,1,0:T(1,128)}), f32[8,1,456]{2,1,0:T(1,128)S(1)}, u32[]{:S(2)}, u32[]{:S(2)}) async-start(f32[8,1,456]{2,1,0:T(1,128)} %reshape.241), calls=%async_computation.1 | async-start | bytes 32768 | tf_op jit(solution)/shard_map/all_to_all | solution.py:210
Sparse Core Ops, SparseCore 0:
  26.9 39.3 reduce-scatter.1

commit v2 on v1

--- a/solution.py
+++ b/solution.py
@@ -52,54 +52,253 @@
     return horner(COS_FIT, w), u * horner(SIN_FIT, w)
 
 
-def projection_kernel(sites_ref, kinds_ref, miller_ref, beta_ref, wave_ref, out_ref, rows_ref):
-    block = sites_ref.shape[0]
+MESH = pl.DeviceIdType.MESH
+
+
+def greet(peers, axis_sets):
+    barrier = pltpu.get_barrier_semaphore()
+    for count, device_of in axis_sets:
+
+        @pl.loop(1, count)
+        def _(step):
+            pl.semaphore_signal(barrier, inc=1, device_id=device_of(step), device_id_type=MESH)
+
+    pl.semaphore_wait(barrier, peers)
+
+
+def group_peer(groups):
+    band, me = lax.axis_index("band"), lax.axis_index("ga")
+    return lambda step: (band, lax.rem(me + step, groups))
+
+
+def band_peer(bands):
+    band, me = lax.axis_index("band"), lax.axis_index("ga")
+    return lambda step: (lax.rem(band + step, bands), me)
+
+
+def projection_kernel(
+    groups,
+    own,
+    sites_ref,
+    kinds_ref,
+    miller_ref,
+    beta_ref,
+    wave_ref,
+    out_ref,
+    rows_ref,
+    send_ref,
+    recv_ref,
+    send_sem,
+    recv_sem,
+):
+    band, me = lax.axis_index("band"), lax.axis_index("ga")
     width = miller_ref.shape[1]
-    site = sites_ref[...]
-    miller = miller_ref[...]
-    count = site[:, 0:1] * miller[0:1, :] + site[:, 1:2] * miller[1:2, :] + site[:, 2:3] * miller[2:3, :]
-    cosine, sine = turn_cos_sin(count, PERIOD)
-    kinds = kinds_ref[...]
-    masks = [kinds == s for s in range(1, SPECIES)]
-    for i in range(NH):
-        radial = jnp.broadcast_to(beta_ref[i : i + 1, :], (block, width))
-        for s in range(1, SPECIES):
-            radial = jnp.where(masks[s - 1], beta_ref[s * NH + i : s * NH + i + 1, :], radial)
-        if ELL[i] == 0:
-            real, imag = radial * cosine, -(radial * sine)
-        elif ELL[i] == 1:
-            real, imag = -(radial * sine), -(radial * cosine)
-        else:
-            real, imag = -(radial * cosine), radial * sine
-        row = (i % HALF) * block
-        col = (i // HALF) * 2 * width
-        rows_ref[row : row + block, col : col + width] = real.astype(BF16)
-        rows_ref[row : row + block, col + width : col + 2 * width] = imag.astype(BF16)
-    result = jnp.dot(rows_ref[...], wave_ref[...], preferred_element_type=F32)
-    out_ref[...] = result.reshape(HALF, block, result.shape[1])
-
-
-def project(sites, kinds, miller, beta_table, wave_matrix):
+    steps, _, block, cols = send_ref.shape
+    ratio = block // own
+    greet(groups - 1, [(groups, group_peer(groups))])
+
+    def copy_to(index, part, target):
+        return pltpu.make_async_remote_copy(
+            src_ref=send_ref.at[index, :, pl.ds(pl.multiple_of(part * own, own), own), :],
+            dst_ref=recv_ref.at[me],
+            send_sem=send_sem.at[target],
+            recv_sem=recv_sem.at[me],
+            device_id=(band, target),
+            device_id_type=MESH,
+        )
+
+    @pl.loop(0, steps)
+    def _(step):
+        index = lax.rem(me // ratio + 1 + step, steps)
+        start = pl.multiple_of(index * block, block)
+        site = sites_ref[pl.ds(start, block), :]
+        kinds = kinds_ref[pl.ds(start, block), :]
+        miller = miller_ref[...]
+        count = site[:, 0:1] * miller[0:1, :] + site[:, 1:2] * miller[1:2, :] + site[:, 2:3] * miller[2:3, :]
+        cosine, sine = turn_cos_sin(count, PERIOD)
+        masks = [kinds == s for s in range(1, SPECIES)]
+        for i in range(NH):
+            radial = jnp.broadcast_to(beta_ref[i : i + 1, :], (block, width))
+            for s in range(1, SPECIES):
+                radial = jnp.where(masks[s - 1], beta_ref[s * NH + i : s * NH + i + 1, :], radial)
+            if ELL[i] == 0:
+                real, imag = radial * cosine, -(radial * sine)
+            elif ELL[i] == 1:
+                real, imag = -(radial * sine), -(radial * cosine)
+            else:
+                real, imag = -(radial * cosine), radial * sine
+            row = (i % HALF) * block
+            col = (i // HALF) * 2 * width
+            rows_ref[row : row + block, col : col + width] = real.astype(BF16)
+            rows_ref[row : row + block, col + width : col + 2 * width] = imag.astype(BF16)
+        result = jnp.dot(rows_ref[...], wave_ref[...], preferred_element_type=F32)
+        send_ref[index] = result.reshape(HALF, block, cols)
+        for part in range(ratio):
+            target = index * ratio + part
+
+            @pl.when(target != me)
+            def _():
+                copy_to(index, part, target).start()
+
+    total = send_ref[me // ratio, :, pl.ds(pl.multiple_of(lax.rem(me, ratio) * own, own), own), :]
+    for step in range(1, groups):
+        source = lax.rem(me + step, groups)
+        pltpu.make_async_remote_copy(
+            src_ref=send_ref.at[0, :, pl.ds(0, own), :],
+            dst_ref=recv_ref.at[source],
+            send_sem=send_sem.at[source],
+            recv_sem=recv_sem.at[source],
+            device_id=(band, source),
+            device_id_type=MESH,
+        ).wait_recv()
+        total = total + recv_ref[source]
+    out_ref[...] = total
+
+    @pl.loop(1, groups)
+    def _(step):
+        target = lax.rem(me + step, groups)
+        copy_to(0, 0, target).wait_send()
+
+
+def project(sites, kinds, miller, beta_table, wave_matrix, groups):
     atoms = sites.shape[0]
     width = miller.shape[1]
     cols = wave_matrix.shape[1]
-    block = math.gcd(atoms, 32)
-    whole = lambda a: pl.BlockSpec(a.shape, lambda b: (0, 0))
+    own = atoms // groups
+    block = own * max(1, 32 // own)
+    steps = atoms // block
     return pl.pallas_call(
-        projection_kernel,
-        grid=(atoms // block,),
-        in_specs=[
-            pl.BlockSpec((block, 3), lambda b: (b, 0)),
-            pl.BlockSpec((block, 1), lambda b: (b, 0)),
-            whole(miller),
-            whole(beta_table),
-            whole(wave_matrix),
+        functools.partial(projection_kernel, groups, own),
+        in_specs=[pl.BlockSpec(memory_space=pltpu.VMEM)] * 5,
+        out_specs=pl.BlockSpec(memory_space=pltpu.VMEM),
+        out_shape=jax.ShapeDtypeStruct((HALF, own, cols), F32),
+        scratch_shapes=[
+            pltpu.VMEM((HALF * block, 4 * width), BF16),
+            pltpu.VMEM((steps, HALF, block, cols), F32),
+            pltpu.VMEM((groups, HALF, own, cols), F32),
+            pltpu.SemaphoreType.DMA((groups,)),
+            pltpu.SemaphoreType.DMA((groups,)),
         ],
-        out_specs=pl.BlockSpec((HALF, block, cols), lambda b: (0, b, 0)),
-        out_shape=jax.ShapeDtypeStruct((HALF, atoms, cols), F32),
-        scratch_shapes=[pltpu.VMEM((HALF * block, 4 * width), BF16)],
+        compiler_params=pltpu.CompilerParams(collective_id=0, has_side_effects=True),
         name="project",
     )(sites, kinds, miller, beta_table, wave_matrix)
+
+
+def becsum_kernel(bands, groups, part_ref, out_ref, recv_ref, sum_ref, band_send, band_recv, send_sem, recv_sem):
+    band, me = lax.axis_index("band"), lax.axis_index("ga")
+    to_band, to_group = band_peer(bands), group_peer(groups)
+    greet(bands + groups - 2, [(bands, to_band), (groups, to_group)])
+
+    def band_copy(step, slot):
+        return pltpu.make_async_remote_copy(
+            src_ref=part_ref,
+            dst_ref=recv_ref.at[slot],
+            send_sem=band_send.at[step],
+            recv_sem=band_recv.at[slot],
+            device_id=to_band(step),
+            device_id_type=MESH,
+        )
+
+    def group_copy(step, slot):
+        return pltpu.make_async_remote_copy(
+            src_ref=sum_ref,
+            dst_ref=out_ref.at[slot],
+            send_sem=send_sem.at[step],
+            recv_sem=recv_sem.at[slot],
+            device_id=to_group(step),
+            device_id_type=MESH,
+        )
+
+    for step in range(1, bands):
+        band_copy(step, band).start()
+    recv_ref[band] = part_ref[...]
+    for step in range(1, bands):
+        band_copy(step, lax.rem(band + step, bands)).wait_recv()
+    total = recv_ref[0]
+    for source in range(1, bands):
+        total = total + recv_ref[source]
+    sum_ref[...] = total
+    for step in range(1, groups):
+        group_copy(step, me).start()
+    out_ref[me] = total
+    for step in range(1, bands):
+        band_copy(step, band).wait_send()
+    for step in range(1, groups):
+        group_copy(step, lax.rem(me + step, groups)).wait_recv()
+    for step in range(1, groups):
+        group_copy(step, me).wait_send()
+
+
+def gather_becsum(part, bands, groups):
+    return pl.pallas_call(
+        functools.partial(becsum_kernel, bands, groups),
+        in_specs=[pl.BlockSpec(memory_space=pltpu.VMEM)],
+        out_specs=pl.BlockSpec(memory_space=pltpu.VMEM),
+        out_shape=jax.ShapeDtypeStruct((groups,) + part.shape, F32),
+        scratch_shapes=[
+            pltpu.VMEM((bands,) + part.shape, F32),
+            pltpu.VMEM(part.shape, F32),
+            pltpu.SemaphoreType.DMA((bands,)),
+            pltpu.SemaphoreType.DMA((bands,)),
+            pltpu.SemaphoreType.DMA((groups,)),
+            pltpu.SemaphoreType.DMA((groups,)),
+        ],
+        compiler_params=pltpu.CompilerParams(collective_id=1, has_side_effects=True),
+        name="gather_becsum",
+    )(part)
+
+
+def sticks_kernel(bands, groups, part_ref, out_ref, send_sem, recv_sem):
+    band, me = lax.axis_index("band"), lax.axis_index("ga")
+    place = band * groups + me
+    devices = bands * groups
+
+    def peer(step):
+        other = lax.rem(place + step, devices)
+        return other // groups, lax.rem(other, groups)
+
+    greet(devices - 1, [(devices, peer)])
+
+    def copy(step, slot):
+        target = peer(step)
+        return pltpu.make_async_remote_copy(
+            src_ref=part_ref.at[target[1]],
+            dst_ref=out_ref.at[slot],
+            send_sem=send_sem.at[step],
+            recv_sem=recv_sem.at[slot],
+            device_id=target,
+            device_id_type=MESH,
+        )
+
+    @pl.loop(1, devices)
+    def _(step):
+        copy(step, place).start()
+
+    out_ref[place] = part_ref[me]
+
+    @pl.loop(1, devices)
+    def _(step):
+        copy(step, lax.rem(place + step, devices)).wait_recv()
+
+    @pl.loop(1, devices)
+    def _(step):
+        copy(step, place).wait_send()
+
+
+def exchange_sticks(part, bands, groups):
+    devices = bands * groups
+    return pl.pallas_call(
+        functools.partial(sticks_kernel, bands, groups),
+        in_specs=[pl.BlockSpec(memory_space=pltpu.VMEM)],
+        out_specs=pl.BlockSpec(memory_space=pltpu.VMEM),
+        out_shape=jax.ShapeDtypeStruct((devices,) + part.shape[1:], F32),
+        scratch_shapes=[
+            pltpu.SemaphoreType.DMA((devices,)),
+            pltpu.SemaphoreType.DMA((devices,)),
+        ],
+        compiler_params=pltpu.CompilerParams(collective_id=2, has_side_effects=True),
+        name="exchange_sticks",
+    )(part)
 
 
 def dense_kernel(weights_ref, table_ref, sites_ref, points_ref, out_ref):
@@ -171,8 +370,7 @@
     wave_matrix = jnp.concatenate(
         [jnp.concatenate([wave_t, empty], axis=1), jnp.concatenate([empty, wave_t], axis=1)], axis=0
     )
-    pieces = project(sites, atom_kinds[:, None], wave_miller.astype(F32), beta_table, wave_matrix)
-    own = lax.psum_scatter(pieces, "ga", scatter_dimension=1, tiled=True)
+    own = project(sites, atom_kinds[:, None], wave_miller.astype(F32), beta_table, wave_matrix, groups)
     own_atoms = own.shape[1]
     blocks = own.reshape(HALF, own_atoms, 2, wave_t.shape[1]).transpose(1, 2, 0, 3)
     blocks = blocks.reshape(own_atoms, NH, wave_t.shape[1])
@@ -180,7 +378,7 @@
     square = jnp.einsum("aic,ajc->aij", blocks * occupied[None, None, :], blocks, precision=highest)
     factors = np.where(PAIR_FIRST == PAIR_SECOND, 1.0, 2.0).astype(np.float32)
     partial_value = square.reshape(own_atoms, NH * NH)[:, PAIR_FIRST * NH + PAIR_SECOND] * factors[None, :]
-    becsum = lax.all_gather(lax.psum(partial_value, "band"), "ga", axis=0, tiled=True)
+    becsum = gather_becsum(partial_value, bands, groups).reshape(atoms, -1)
     weights = augment_weights(becsum, atom_kinds)
 
     column_x = lax.axis_index("band") * column_block + stick_columns // NY
@@ -194,21 +392,19 @@
         ]
     ).astype(F32)
     aug = dense(weights, aug_table, sites, points).reshape(2, slots, NZ)
+    lines = aug.transpose(1, 0, 2).reshape(slots, 2 * NZ)
     cos_z, sin_z = table_of(np.arange(NZ), np.arange(NZ), NZ)
-    both = jnp.dot(aug.reshape(2 * slots, NZ), np.concatenate([cos_z, sin_z], axis=1), precision=highest)
-    both = both.reshape(2, slots, 2, NZ)
-    stick_re = both[0, :, 0] - both[1, :, 1]
-    stick_im = both[0, :, 1] + both[1, :, 0]
-    packed = jnp.concatenate(
-        [
-            stick_re.reshape(slots, groups, planes),
-            stick_im.reshape(slots, groups, planes),
-            jnp.broadcast_to(stick_columns.astype(F32)[:, None, None], (slots, groups, 1)),
-        ],
-        axis=2,
-    ).transpose(1, 0, 2)
-    received = lax.all_to_all(packed, "ga", split_axis=0, concat_axis=0, tiled=True)
-    received = lax.all_gather(received.reshape(groups * slots, -1), "band", axis=0, tiled=True)
+    lanes = 128 * (-(-(2 * planes + 1) // 128))
+    spread = np.zeros((2, NZ, groups, lanes), np.float32)
+    spread[0, :, :, :planes] = cos_z.reshape(NZ, groups, planes)
+    spread[1, :, :, :planes] = -sin_z.reshape(NZ, groups, planes)
+    spread[0, :, :, planes : 2 * planes] = sin_z.reshape(NZ, groups, planes)
+    spread[1, :, :, planes : 2 * planes] = cos_z.reshape(NZ, groups, planes)
+    packed = jnp.dot(lines, spread.reshape(2 * NZ, groups * lanes), precision=highest)
+    packed = packed.reshape(slots, groups, lanes).transpose(1, 0, 2)
+    at_column = jnp.arange(lanes)[None, None, :] == 2 * planes
+    packed = jnp.where(at_column, stick_columns.astype(F32)[None, :, None], packed)
+    received = exchange_sticks(packed, bands, groups).reshape(bands * groups * slots, lanes)
     return finish(received, planes, y_block, column_block, groups * slots)
 
 

time: 150 us -> 89.6 us (0.60)
  waiting for transfers between devices: 43 us -> 0 us
  blocking collectives: 42 us -> 0 us
  Pallas kernels: 19.3 us -> 53.8 us
  between operations: 13.7 us -> 0.24 us
  other arithmetic: 10.2 us -> 14.6 us
  starting transfers between devices: 3.34 us -> 0 us
    reduce_scatter x1 -> x0, waiting for transfers between devices: 38.3 us -> none  [on_device(): own = lax.psum_scatter(pieces, 'ga', scatter_dimension=1, tiled=True)]
    pallas_call x1 -> x3, Pallas kernels: 12 us -> 46.4 us  [the longest x1 20.6 us: project(): pl.pallas_call(functools.partial(projection_kernel, groups, own), in_spec...]
    all_gather x2 -> x0, blocking collectives: 23 us -> none  [the longest x1 13.7 us: on_device(): lax.all_gather(received.reshape(groups * slots, -1), 'band', axis=0, tile...]
    psum x1 -> x0, blocking collectives: 19 us -> none  [on_device(): lax.psum(partial_value, 'band')]
    all_to_all x1 -> x0, waiting for transfers between devices: 4.67 us -> none  [on_device(): lax.all_to_all(packed, 'ga', split_axis=0, concat_axis=0, tiled=True)]
    all_to_all x1 -> x0, starting transfers between devices: 3.34 us -> none  [on_device(): lax.all_to_all(packed, 'ga', split_axis=0, concat_axis=0, tiled=True)]
    another operation x2, other arithmetic: 0.04 us -> 1.95 us
  transfers between devices with their start and end apart: 2 -> 0, of which waited for: 2 -> 0; matrix products, arithmetic and copies ran while one was open for 1% -> 0% of each run, Pallas kernels for 0% -> 0%
where the time goes in v2:
time: 89.6 us; the launch traced here: 88.8 us
  Pallas kernels  53.8 us (60%)
  other arithmetic  14.6 us (16%)
  local copies, waits for them, and re-layouts  14.2 us (16%)
  matrix products  6.03 us (7%)
    pallas_call x1, Pallas kernels, project(): pl.pallas_call(functools.partial(projection_kernel, groups, own), in_spec...  20.6 us
    pallas_call x1, Pallas kernels, gather_becsum(): pl.pallas_call(functools.partial(becsum_kernel, bands, groups), in_specs=...  15.6 us
    pallas_call x1, Pallas kernels, exchange_sticks(): pl.pallas_call(functools.partial(sticks_kernel, bands, groups), in_specs=...  10.2 us
    pallas_call x1, Pallas kernels, dense(): pl.pallas_call(dense_kernel, grid=(cols // tile,), in_specs=[pl.BlockSpec...  7.37 us
    another operation x1, local copies, waits for them, and re-layouts, finish(): return jnp.stack([out_re, out_im])  4.42 us
    concatenate x2, local copies, waits for them, and re-layouts, augment_weights(): kinds = jnp.concatenate([atom_kinds, atom_kinds])[:, None]  2.16 us
    another operation x2, other arithmetic  1.95 us

profile of v2, /device:TPU:0, one launch (start us, length us, event | category | flops | bytes accessed | tf_op | source)
XLA Modules:
  0.0 88.8 jit_solution(1014107387184599452)
XLA Ops:
  0.0 0.8 pad_maximum_fusion.12
  0.8 0.7 fusion.81
  1.6 0.7 constant_dynamic-update-slice_fusion.1
  2.3 0.7 constant_dynamic-update-slice_fusion
  3.0 0.8 convert_multiply_fusion
  3.7 0.7 pad_clamp_fusion
  4.4 0.1 mul.303
  4.5 0.1 stack_reshape.9
  4.6 0.1 mul.304
  4.6 0.1 stack_reshape.10
  4.7 0.1 stack_reshape.11
  4.8 0.6 add_convert_fusion.points_ref
  5.5 1.3 %convert_element_type.43.miller_ref = f32[3,1024]{1,0:T(4,128)} convert(s32[3,1024]{1,0:T(4,128)} %param.17) | non-fusion elementwise | flops 3072 | bytes 24576 | tf_op jit(solution)/shard_map/convert_element_type | solution.py:373
  6.8 0.8 fusion.80
  7.6 0.8 copy.56
  8.4 1.5 %copy.59.kinds_ref = s32[256,1]{1,0:T(8,128)} copy(s32[256,1]{0,1:T(1,128)} %bitcast.49) | data formatting | bytes 2048 | tf_op jit(solution)/shard_map/concatenate | solution.py:339
  9.9 0.9 slice_bitcast_fusion.1
  10.8 0.3 copy.57
  11.1 0.3 copy.58
  11.4 0.3 maximum_bitcast_fusion
  11.7 1.2 %fusion.7.wave_ref = bf16[4096,128]{1,0:T(8,128)(2,1)} fusion(bf16[2048,64]{1,0:T(8,128)(2,1)S(1)} %maximum_bitcast_fusion), kind=kLoop, calls=%fused_computation.15 | loop fusion | flops 4194304 | bytes 1310720 | tf_op jit(solution)/shard_map/concatenate | solution.py:370
  12.9 20.6 %project.1 = f32[9,32,128]{2,1,0:T(8,128)} custom-call(f32[256,3]{1,0:T(8,128)} %bitcast.46, s32[256,1]{1,0:T(8,128)} %copy.59.kinds_ref, f32[3,1024]{1,0:T(4,128)} %convert_element_type.43.miller_ref, f32[72,1024]{1,0:T(8,128)} %beta_ref.1, bf16[4096,128]{1,0:T(8,128)(2,1)} %fusion.7.wave_ref), custom_call_target="tpu_custom_call" | custom-call | tf_op jit(solution)/shard_map/project/pallas_call | solution.py:170
  33.5 0.0 copy-start.2
  33.5 1.1 %reshape.222 = f32[9,32,2,64]{3,2,1,0:T(2,128)S(1)} reshape(f32[9,32,128]{2,1,0:T(8,128)} %project.1) | data formatting | bytes 294912 | tf_op jit(solution)/shard_map/reshape | solution.py:375
  34.7 0.0 copy-start.1
  34.7 1.1 %fusion.12 = f32[32,18,18]{2,1,0:T(8,128)S(1)} fusion(f32[32,18,64]{2,0,1:T(8,128)S(1)} %bitcast.43, f32[32,18,64]{2,0,1:T(8,128)S(1)} %broadcast_multiply_fusion), kind=kOutput, calls=%fused_computation.24 | convolution fusion | flops 7962624 | bytes 336384 | tf_op jit(solution)/shard_map/aic,ajc->aij/dot_general | solution.py:378
  35.8 0.1 reshape.240
  36.0 0.1 copy.70
  36.1 0.7 gather_fusion
  36.8 0.1 copy.64
  36.8 0.0 copy-done.2
  36.8 0.6 multiply_bitcast_fusion.part_ref
  37.5 15.6 %gather_becsum.1 = f32[8,32,171]{2,1,0:T(8,128)} custom-call(f32[32,171]{1,0:T(8,128)} %multiply_bitcast_fusion.part_ref), custom_call_target="tpu_custom_call" | custom-call | tf_op jit(solution)/shard_map/gather_becsum/pallas_call | solution.py:233
  53.1 0.0 copy-done.1
  53.1 1.0 %fusion.17 = bf16[256,171]{1,0:T(8,128)(2,1)S(1)} fusion(f32[8,32,171]{2,1,0:T(8,128)} %gather_becsum.1, pred[171]{0:T(512)(128)(4,1)S(1)} %copy-done.1), kind=kLoop, calls=%fused_computation.34 | loop fusion | flops 131328 | bytes 262827 | tf_op jit(solution)/shard_map/convert.1
  54.1 1.0 %fusion.15 = bf16[256,171]{1,0:T(8,128)(2,1)S(1)} fusion(f32[8,32,171]{2,1,0:T(8,128)} %gather_becsum.1, pred[171]{0:T(512)(128)(4,1)S(1)} %copy-done.1), kind=kLoop, calls=%fused_computation.32 | loop fusion | flops 43776 | bytes 262827 | tf_op jit(solution)/shard_map/convert
  55.1 0.9 broadcast_select_fusion.3
  56.0 1.3 %pad_maximum_fusion.8.weights_ref = bf16[512,684]{1,0:T(8,128)(2,1)} fusion(bf16[512,171]{1,0:T(8,128)(2,1)S(1)} %get-tuple-element.8, bf16[512,171]{1,0:T(8,128)(2,1)S(1)} %get-tuple-element.7, bf16[512,171]{1,0:T(8,128)(2,1)S(1)} %get-tuple-element.6, bf16[512,171]{1,0:T(8,128)(2,1)S(1)} %get-tuple-element.5), kind=kLoop, calls=%fused_computation.16 | loop fusion | flops 2801664 | bytes 1400832 | tf_op jit(solution)/shard_map/concatenate | solution.py:341
  57.3 0.0 copy-start
  57.3 7.4 %dense.1 = f32[2,1792]{1,0:T(2,128)} custom-call(bf16[512,684]{1,0:T(8,128)(2,1)} %pad_maximum_fusion.8.weights_ref, bf16[684,1792]{1,0:T(8,128)(2,1)} %table_ref.1, f32[256,3]{1,0:T(8,128)} %bitcast.47, f32[3,1792]{1,0:T(4,128)} %add_convert_fusion.points_ref), custom_call_target="tpu_custom_call" | custom-call | tf_op jit(solution)/shard_map/dense/pallas_call | solution.py:319
  64.6 0.8 reshape.226
  65.4 0.1 reshape.237
  65.5 0.0 copy-done
  65.5 1.6 %fusion.6.part_ref = f32[8,8,128]{2,1,0:T(8,128)} fusion(f32[8,448,1]{1,0,2:T(8,128)S(1)} %reshape.237, f32[8,128,448]{1,2,0:T(8,128)S(1)} %copy-done, f32[8]{0:T(128)S(1)} %get-tuple-element.28, pred[128]{0:T(512)(128)(4,1)S(1)} %iota_compare_fusion.2), kind=kOutput, calls=%fused_computation.14 | convolution fusion | flops 44048384 | bytes 1882272 | tf_op jit(solution)/shard_map/dot_general | solution.py:403
  67.1 10.2 %exchange_sticks.1 = f32[32,8,128]{2,1,0:T(8,128)} custom-call(f32[8,8,128]{2,1,0:T(8,128)} %fusion.6.part_ref), custom_call_target="tpu_custom_call" | custom-call | tf_op jit(solution)/shard_map/exchange_sticks/pallas_call | solution.py:290
  77.3 1.0 %slice.24 = f32[256,1]{1,0:T(8,128)S(1)} slice(f32[256,128]{1,0:T(8,128)} %bitcast.44), slice={[0:256], [56:57]} | slice | bytes 2048 | tf_op jit(solution)/shard_map/slice | solution.py:413
  78.3 0.1 copy.71
  78.4 0.1 fusion.67
  78.6 1.1 %slice_select_fusion.1 = (f32[256,28]{1,0:T(8,128)S(1)}, f32[256,28]{1,0:T(8,128)S(1)}) fusion(f32[256,128]{1,0:T(8,128)} %bitcast.45, pred[256]{0:T(512)(128)(4,1)S(1)} %compare_reduce_fusion), kind=kLoop, calls=%fused_computation.68 | loop fusion | flops 14336 | bytes 114944 | tf_op jit(solution)/shard_map/jit(_where)/select_n | solution.py:415
  79.7 0.1 copy.67
  79.8 0.1 copy.68
  79.9 0.3 fusion.45
  80.2 0.5 multiply_subtract_fusion
  80.7 1.7 %fusion.5 = f32[1,28,60,240]{3,2,1,0:T(8,128)S(1)} fusion(f32[256,28,60]{0,2,1:T(8,128)S(1)} %get-tuple-element.10, f32[256,28,60]{0,2,1:T(8,128)S(1)} %get-tuple-element.9, f32[256,240]{0,1:T(8,128)S(1)} %get-tuple-element.19, f32[256,240]{0,1:T(8,128)S(1)} %get-tuple-element.18), kind=kOutput, calls=%fused_computation.12 | convolution fusion | flops 1239613440 | bytes 5544960 | tf_op jit(solution)/shard_map/dot_general | solution.py:430
  82.4 1.7 %fusion.4 = f32[1,28,60,240]{3,2,1,0:T(8,128)S(1)} fusion(f32[256,28,60]{0,2,1:T(8,128)S(1)} %get-tuple-element.10, f32[256,28,60]{0,2,1:T(8,128)S(1)} %get-tuple-element.9, f32[256,240]{0,1:T(8,128)S(1)} %get-tuple-element.17, f32[256,240]{0,1:T(8,128)S(1)} %get-tuple-element.19), kind=kOutput, calls=%fused_computation.11 | convolution fusion | flops 1239613440 | bytes 5544960 | tf_op jit(solution)/shard_map/dot_general | solution.py:429
  84.1 0.3 pad_maximum_fusion.1
  84.4 4.4 %copy.69 = f32[2,28,60,240]{3,0,2,1:T(2,128)} copy(f32[2,28,60,240]{3,2,1,0:T(8,128)S(1)} %pad_maximum_fusion.1) | data formatting | bytes 6451200 | tf_op jit(solution)/shard_map/stack | solution.py:431
  (12 shorter events, 0.2 us)
Async XLA Ops:
  33.5 3.3 %copy-start.2 = (f32[171]{0:T(256)S(1)}, f32[171]{0:T(256)}, u32[]{:S(2)}) copy-start(f32[171]{0:T(256)} %constant.137) | copy-start | bytes 2056
  34.7 18.5 %copy-start.1 = (pred[171]{0:T(512)(128)(4,1)S(1)}, pred[171]{0:T(512)(128)(4,1)}, u32[]{:S(2)}) copy-start(pred[171]{0:T(512)(128)(4,1)} %constant.129.clone) | copy-start | bytes 517
  57.3 8.3 %copy-start = (f32[8,128,448]{1,2,0:T(8,128)S(1)}, f32[8,128,448]{1,2,0:T(8,128)}, u32[]{:S(2)}) copy-start(f32[8,128,448]{1,2,0:T(8,128)} %constant.139) | copy-start | bytes 5505028

commit v3 on v1

v3 whole, which is shorter than its diff:
```python
import functools
import math

import jax
import jax.numpy as jnp
import numpy as np
from jax import lax
from jax.experimental import pallas as pl
from jax.experimental.pallas import tpu as pltpu
from jax.sharding import PartitionSpec as P

NX = 240
NY = 240
NZ = 224
NH = 18
HALF = NH // 2
SPECIES = 4

PERIOD = math.lcm(NX, NY, NZ)
STEP_X = PERIOD // NX
STEP_Y = PERIOD // NY
STEP_Z = PERIOD // NZ
ELL = np.array([0, 0] + [1] * 6 + [2] * 10)
PAIR_FIRST, PAIR_SECOND = np.triu_indices(NH)

highest = lax.Precision.HIGHEST
F32 = jnp.float32
BF16 = jnp.bfloat16


def fit_even(func, terms):
    nodes = 0.125 * (1.0 + np.cos(np.pi * (np.arange(64) + 0.5) / 64))
    scaled = np.polynomial.chebyshev.Chebyshev.fit(nodes, func(np.sqrt(nodes)), terms - 1, domain=[0, 0.25])
    return [float(c) for c in scaled.convert(kind=np.polynomial.Polynomial).coef]


COS_FIT = fit_even(lambda u: np.cos(2 * np.pi * u), 7)
SIN_FIT = fit_even(lambda u: np.sin(2 * np.pi * u) / u, 6)


def horner(coefs, w):
    total = jnp.full_like(w, coefs[-1])
    for c in coefs[-2::-1]:
        total = total * w + c
    return total


def turn_cos_sin(count, period):
    rest = count - jnp.round(count * (1.0 / period)) * period
    u = rest * (1.0 / period)
    w = u * u
    return horner(COS_FIT, w), u * horner(SIN_FIT, w)


MESH = pl.DeviceIdType.MESH


def greet(peers, axis_sets):
    barrier = pltpu.get_barrier_semaphore()
    for count, device_of in axis_sets:

        @pl.loop(1, count)
        def _(step):
            pl.semaphore_signal(barrier, inc=1, device_id=device_of(step), device_id_type=MESH)

    pl.semaphore_wait(barrier, peers)


def up(value, unit):
    return -(-value // unit) * unit


def split(value):
    high = value.astype(BF16)
    return high, (value - high.astype(F32)).astype(BF16)


def mega_kernel(
    bands,
    groups,
    waves_ref,
    occ_ref,
    beta_ref,
    miller_ref,
    kinds_ref,
    site_ref,
    columns_ref,
    signs_ref,
    table_hbm,
    spread_hbm,
    out_ref,
    small_ref,
    site_t_ref,
    wave_ref,
    rows_ref,
    send_ref,
    recv_ref,
    phase_ref,
    total_ref,
    part_ref,
    band_ref,
    pair_ref,
    pack_ref,
    all_ref,
    weights_ref,
    table_ref,
    spread_ref,
    aug_ref,
    lines_ref,
    stick_ref,
    rs_send,
    rs_recv,
    band_send,
    band_recv,
    ga_send,
    ga_recv,
    dev_send,
    dev_recv,
    local_sem,
):
    band, me = lax.axis_index("band"), lax.axis_index("ga")
    devices = bands * groups
    place = band * groups + me
    atoms = site_ref.shape[1]
    own = atoms // groups
    width = miller_ref.shape[1]
    nb = waves_ref.shape[1]
    slots = columns_ref.shape[0]
    steps, _, block, cols = send_ref.shape
    ratio = block // own
    points = slots * NZ
    tile = phase_ref.shape[-1]
    planes = NZ // groups
    lanes = stick_ref.shape[-1]
    pairs = len(PAIR_FIRST)

    table_copy = pltpu.make_async_copy(table_hbm, table_ref, local_sem.at[0])
    spread_copy = pltpu.make_async_copy(spread_hbm, spread_ref, local_sem.at[1])
    table_copy.start()
    spread_copy.start()

    def peer(step):
        other = lax.rem(place + step, devices)
        return other // groups, lax.rem(other, groups)

    greet(devices - 1, [(devices, peer)])

    small_ref[...] = jnp.zeros_like(small_ref)
    small_ref[0:1, :] = site_ref[0:1, :].astype(F32) * STEP_X
    small_ref[1:2, :] = site_ref[1:2, :].astype(F32) * STEP_Y
    small_ref[2:3, :] = site_ref[2:3, :].astype(F32) * STEP_Z
    small_ref[3:4, :] = kinds_ref[...].astype(F32)
    small_ref[4:5, 0:nb] = occ_ref[...]
    small_ref[4:5, nb : 2 * nb] = occ_ref[...]
    site_t_ref[...] = jnp.swapaxes(small_ref[...], 0, 1)

    wave_ref[...] = jnp.zeros_like(wave_ref)
    re, im = waves_ref[0], waves_ref[1]
    for h in range(2):
        r, c = 2 * nb * h, 2 * width * h
        wave_ref[r : r + nb, c : c + width] = re
        wave_ref[r : r + nb, c + width : c + 2 * width] = im
        wave_ref[r + nb : r + 2 * nb, c : c + width] = im
        wave_ref[r + nb : r + 2 * nb, c + width : c + 2 * width] = -re

    def rs_copy(index, part, target, slot):
        return pltpu.make_async_remote_copy(
            src_ref=send_ref.at[index, :, pl.ds(pl.multiple_of(part * own, own), own), :],
            dst_ref=recv_ref.at[slot],
            send_sem=rs_send.at[target],
            recv_sem=rs_recv.at[slot],
            device_id=(band, target),
            device_id_type=MESH,
        )

    @pl.loop(0, steps)
    def _(step):
        index = lax.rem(me // ratio + 1 + step, steps)
        start = pl.multiple_of(index * block, block)
        site = site_t_ref[pl.ds(start, block), :]
        kinds = site[:, 3:4]
        miller = miller_ref[...].astype(F32)
        count = site[:, 0:1] * miller[0:1, :] + site[:, 1:2] * miller[1:2, :] + site[:, 2:3] * miller[2:3, :]
        cosine, sine = turn_cos_sin(count, PERIOD)
        masks = [kinds == float(s) for s in range(1, SPECIES)]
        for i in range(NH):
            radial = jnp.broadcast_to(beta_ref[i : i + 1, :], (block, width))
            for s in range(1, SPECIES):
                radial = jnp.where(masks[s - 1], beta_ref[s * NH + i : s * NH + i + 1, :], radial)
            if ELL[i] == 0:
                real, imag = radial * cosine, -(radial * sine)
            elif ELL[i] == 1:
                real, imag = -(radial * sine), -(radial * cosine)
            else:
                real, imag = -(radial * cosine), radial * sine
            row = (i % HALF) * block
            col = (i // HALF) * 2 * width
            rows_ref[row : row + block, col : col + width] = real.astype(BF16)
            rows_ref[row : row + block, col + width : col + 2 * width] = imag.astype(BF16)
        result = lax.dot_general(
            rows_ref[...], wave_ref[...], (((1,), (1,)), ((), ())), preferred_element_type=F32
        )
        send_ref[index] = result.reshape(HALF, block, cols)
        for part in range(ratio):
            target = index * ratio + part

            @pl.when(target != me)
            def _():
                rs_copy(index, part, target, me).start()

    @pl.loop(0, points // tile)
    def _(step):
        point = step * tile + lax.broadcasted_iota(jnp.int32, (1, tile), 1)
        x_row = jnp.zeros((1, tile), F32)
        y_row = jnp.zeros((1, tile), F32)
        z_row = point.astype(F32)
        for t in range(slots):
            column = columns_ref[t]
            x = band * (NX // bands) + lax.div(column, NY)
            y = lax.rem(column, NY)
            inside = point >= t * NZ
            x_row = jnp.where(inside, x.astype(F32), x_row)
            y_row = jnp.where(inside, y.astype(F32), y_row)
            z_row = jnp.where(inside, (point - t * NZ).astype(F32), z_row)
        count = site_t_ref[:, 0:1] * x_row + site_t_ref[:, 1:2] * y_row + site_t_ref[:, 2:3] * z_row
        cosine, sine = turn_cos_sin(count, PERIOD)
        phase_ref[step, 0] = cosine
        phase_ref[step, 1] = sine

    total = send_ref[me // ratio, :, pl.ds(pl.multiple_of(lax.rem(me, ratio) * own, own), own), :]
    for step in range(1, groups):
        source = lax.rem(me + step, groups)
        rs_copy(0, 0, source, source).wait_recv()
        total = total + recv_ref[source]

    total_ref[...] = jnp.zeros_like(total_ref)
    total_ref[0 : HALF * own, :] = total.reshape(HALF * own, cols)
    turned = jnp.swapaxes(total_ref[...], 0, 1)
    becp = jnp.concatenate([turned[0 : 2 * nb, : HALF * own], turned[2 * nb :, : HALF * own]], axis=1)
    scaled = becp * site_t_ref[0 : 2 * nb, 4:5]
    part_ref[...] = jnp.zeros_like(part_ref)
    for d in range(NH):
        size = (NH - d) * own
        product = scaled[:, :size] * becp[:, d * own :]
        part_ref[d : d + 1, 0:size] = jnp.sum(product, axis=0, keepdims=True)

    def band_copy(step, slot):
        return pltpu.make_async_remote_copy(
            src_ref=part_ref,
            dst_ref=band_ref.at[slot],
            send_sem=band_send.at[step],
            recv_sem=band_recv.at[slot],
            device_id=(lax.rem(band + step, bands), me),
            device_id_type=MESH,
        )

    for step in range(1, bands):
        band_copy(step, band).start()
    band_ref[band] = part_ref[...]
    for step in range(1, bands):
        band_copy(step, lax.rem(band + step, bands)).wait_recv()
    summed = band_ref[0]
    for source in range(1, bands):
        summed = summed + band_ref[source]

    pair_ref[...] = jnp.zeros_like(pair_ref)
    begin = 0
    for i in range(NH):
        pair_ref[begin : begin + NH - i, :] = summed[: NH - i, i * own : (i + 1) * own]
        begin += NH - i
    chunk = pack_ref.shape[0]
    chunks = pack_ref.shape[1] // own
    pack_ref[...] = jnp.concatenate(
        [pair_ref[q * chunk : (q + 1) * chunk, :] for q in range(chunks)], axis=1
    )

    def ga_copy(step, slot):
        return pltpu.make_async_remote_copy(
            src_ref=pack_ref,
            dst_ref=all_ref.at[slot],
            send_sem=ga_send.at[step],
            recv_sem=ga_recv.at[slot],
            device_id=(band, lax.rem(me + step, groups)),
            device_id_type=MESH,
        )

    for step in range(1, groups):
        ga_copy(step, me).start()
    all_ref[me] = pack_ref[...]
    for step in range(1, groups):
        ga_copy(step, lax.rem(me + step, groups)).wait_recv()
    becsum = jnp.concatenate(
        [
            jnp.concatenate([all_ref[g, :, q * own : (q + 1) * own] for g in range(groups)], axis=1)
            for q in range(chunks)
        ],
        axis=0,
    )[:pairs]
    even = becsum * signs_ref[:, 0:1]
    odd = becsum * signs_ref[:, 1:2]
    kind_row = small_ref[3:4, :]
    weights_ref[...] = jnp.zeros_like(weights_ref)
    for s in range(SPECIES):
        here = kind_row == float(s)
        weights_ref[s * pairs : (s + 1) * pairs, 0:atoms] = jnp.where(here, even, 0.0)
        weights_ref[s * pairs : (s + 1) * pairs, atoms : 2 * atoms] = jnp.where(here, odd, 0.0)
    weights = jnp.swapaxes(weights_ref[...], 0, 1).astype(BF16)[:, : SPECIES * pairs]

    table_copy.wait()
    for step in range(points // tile):
        coef = jnp.dot(
            weights, table_ref[:, step * tile : (step + 1) * tile], preferred_element_type=F32
        )
        real, imag = coef[:atoms], coef[atoms:]
        cosine, sine = phase_ref[step, 0], phase_ref[step, 1]
        aug_ref[0:1, step * tile : (step + 1) * tile] = jnp.sum(real * cosine + imag * sine, axis=0, keepdims=True)
        aug_ref[1:2, step * tile : (step + 1) * tile] = jnp.sum(imag * cosine - real * sine, axis=0, keepdims=True)

    lines_ref[...] = jnp.zeros_like(lines_ref)
    half = lines_ref.shape[1] // 2
    aug = aug_ref[...]
    for t in range(slots):
        lines_ref[t : t + 1, 0:NZ] = aug[0:1, t * NZ : (t + 1) * NZ]
        lines_ref[t : t + 1, half : half + NZ] = aug[1:2, t * NZ : (t + 1) * NZ]
    high, low = split(lines_ref[...])
    spread_copy.wait()
    lane = lax.broadcasted_iota(jnp.int32, (slots, lanes), 1)
    slot = lax.broadcasted_iota(jnp.int32, (slots, lanes), 0)
    marks = jnp.zeros((slots, lanes), F32)
    for t in range(slots):
        marks = jnp.where(slot == t, columns_ref[t].astype(F32), marks)
    both = jnp.concatenate([high, low], axis=0)
    packed = jnp.dot(both, spread_ref[0], preferred_element_type=F32)
    packed = packed[:slots] + packed[slots:] + jnp.dot(high, spread_ref[1], preferred_element_type=F32)
    for g in range(groups):
        stick_ref[g] = jnp.where(lane == 2 * planes, marks, packed[:, g * lanes : (g + 1) * lanes])

    def stick_copy(step, slot):
        target = peer(step)
        return pltpu.make_async_remote_copy(
            src_ref=stick_ref.at[target[1]],
            dst_ref=out_ref.at[slot],
            send_sem=dev_send.at[step],
            recv_sem=dev_recv.at[slot],
            device_id=target,
            device_id_type=MESH,
        )

    @pl.loop(1, devices)
    def _(step):
        stick_copy(step, place).start()

    out_ref[place] = stick_ref[me]

    @pl.loop(1, devices)
    def _(step):
        stick_copy(step, lax.rem(place + step, devices)).wait_recv()

    for step in range(1, groups):
        target = lax.rem(me + step, groups)
        rs_copy(0, 0, target, me).wait_send()
        ga_copy(step, me).wait_send()
    for step in range(1, bands):
        band_copy(step, band).wait_send()

    @pl.loop(1, devices)
    def _(step):
        stick_copy(step, place).wait_send()


def finish_kernel(bands, groups, received_ref, out_ref, table_ref, turned_ref, angle_ref):
    total, lanes = received_ref.shape
    planes = out_ref.shape[0]
    y_block = out_ref.shape[1]
    y_pad = angle_ref.shape[1]
    band = lax.axis_index("band")
    received = received_ref[...]
    turned = jnp.swapaxes(received, 0, 1)
    turned_ref[...] = turned
    column_row = turned[2 * planes : 2 * planes + 1, :]
    live_row = column_row >= 0.0
    x_row = jnp.floor((column_row + 0.5) * (1.0 / NY))
    y_row = column_row - x_row * NY
    y_values = lax.broadcasted_iota(jnp.int32, (y_pad, total), 0) + band * y_block
    cos_y, sin_y = turn_cos_sin(y_values.astype(F32) * y_row, NY)
    angle_ref[0] = jnp.where(live_row, cos_y, 0.0)
    angle_ref[1] = jnp.where(live_row, sin_y, 0.0)
    column = received[:, 2 * planes : 2 * planes + 1]
    owner = lax.broadcasted_iota(jnp.int32, (total, 1), 0) // (total // bands)
    x = jnp.floor((column + 0.5) * (1.0 / NY)) + owner.astype(F32) * (NX // bands)
    x_values = lax.broadcasted_iota(jnp.int32, (total, 256), 1).astype(F32)
    cos_x, sin_x = turn_cos_sin(x * x_values, NX)
    for part, value in enumerate(split(cos_x)):
        table_ref[part, 0:total, 0:256] = value
        table_ref[part, total : 2 * total, 256:512] = value
    for part, value in enumerate(split(sin_x)):
        table_ref[part, 0:total, 256:512] = value
        table_ref[part, total : 2 * total, 0:256] = -value

    @pl.loop(0, planes)
    def _(z):
        real = turned_ref[pl.ds(z, 1), :]
        imag = turned_ref[pl.ds(planes + z, 1), :]
        cosine, sine = angle_ref[0], angle_ref[1]
        amp = jnp.concatenate([real * cosine - imag * sine, real * sine + imag * cosine], axis=1).astype(BF16)
        result = jnp.dot(amp, table_ref[0], preferred_element_type=F32)
        result = result + jnp.dot(amp, table_ref[1], preferred_element_type=F32)
        out_ref[z, :, 0, :] = result[:y_block, 0:NX]
        out_ref[z, :, 1, :] = result[:y_block, 256 : 256 + NX]


def on_device(
    waves, occupations, beta_table, wave_miller, atom_kinds, atom_sites, aug_table, stick_columns
):
    bands = lax.axis_size("band")
    groups = lax.axis_size("ga")
    devices = bands * groups
    atoms = atom_sites.shape[1]
    slots = stick_columns.shape[0]
    nb = waves.shape[1]
    width = waves.shape[2]
    points = aug_table.shape[1]
    planes = NZ // groups
    pairs = len(PAIR_FIRST)
    own = atoms // groups
    block = own * max(1, 32 // own)
    steps = atoms // block
    cols = 4 * nb
    tile = math.gcd(points, 256)
    lanes = up(2 * planes + 1, 128)
    chunks = 128 // own
    chunk = up(-(-pairs // chunks), 8)

    odd = (ELL[PAIR_FIRST] + ELL[PAIR_SECOND]) % 2 == 1
    factors = np.where(PAIR_FIRST == PAIR_SECOND, 1.0, 2.0)
    signs = np.stack([np.where(odd, 0.0, factors), np.where(odd, -factors, 0.0)], axis=1).astype(np.float32)
    angle = (np.outer(np.arange(NZ), np.arange(NZ)) % NZ) * (2.0 * np.pi / NZ)
    cos_z = np.cos(angle).reshape(NZ, groups, planes)
    sin_z = np.sin(angle).reshape(NZ, groups, planes)
    half = up(NZ, 128)
    spread = np.zeros((2 * half, groups, lanes), np.float32)
    spread[:NZ, :, :planes] = cos_z
    spread[half : half + NZ, :, :planes] = -sin_z
    spread[:NZ, :, planes : 2 * planes] = sin_z
    spread[half : half + NZ, :, planes : 2 * planes] = cos_z
    spread = spread.reshape(2 * half, groups * lanes)
    spread_high = spread.astype(BF16)
    spread_low = (spread - spread_high.astype(np.float32)).astype(BF16)
    vmem = pl.BlockSpec(memory_space=pltpu.VMEM)
    hbm = pl.BlockSpec(memory_space=pl.ANY)
    dma = pltpu.SemaphoreType.DMA
    part_lanes = up(NH * own, 128)
    received = pl.pallas_call(
        functools.partial(mega_kernel, bands, groups),
        in_specs=[vmem] * 6 + [pl.BlockSpec(memory_space=pltpu.SMEM), vmem, hbm, hbm],
        out_specs=vmem,
        out_shape=jax.ShapeDtypeStruct((devices, slots, lanes), F32),
        scratch_shapes=[
            pltpu.VMEM((8, atoms), F32),
            pltpu.VMEM((atoms, 8), F32),
            pltpu.VMEM((cols, 4 * width), BF16),
            pltpu.VMEM((HALF * block, 4 * width), BF16),
            pltpu.VMEM((steps, HALF, block, cols), F32),
            pltpu.VMEM((groups, HALF, own, cols), F32),
            pltpu.VMEM((points // tile, 2, atoms, tile), F32),
            pltpu.VMEM((up(HALF * own, 128), cols), F32),
            pltpu.VMEM((up(NH, 8), part_lanes), F32),
            pltpu.VMEM((bands, up(NH, 8), part_lanes), F32),
            pltpu.VMEM((chunk * chunks, own), F32),
            pltpu.VMEM((chunk, chunks * own), F32),
            pltpu.VMEM((groups, chunk, chunks * own), F32),
            pltpu.VMEM((up(SPECIES * pairs, 128), 2 * atoms), F32),
            pltpu.VMEM(aug_table.shape, BF16),
            pltpu.VMEM((2,) + spread.shape, BF16),
            pltpu.VMEM((8, points), F32),
            pltpu.VMEM((slots, 2 * half), F32),
            pltpu.VMEM((groups, slots, lanes), F32),
            dma((groups,)),
            dma((groups,)),
            dma((bands,)),
            dma((bands,)),
            dma((groups,)),
            dma((groups,)),
            dma((devices,)),
            dma((devices,)),
            dma((2,)),
        ],
        compiler_params=pltpu.CompilerParams(collective_id=0, has_side_effects=True),
        name="slots",
    )(
        waves,
        occupations[None, :],
        beta_table,
        wave_miller,
        atom_kinds[None, :],
        atom_sites,
        stick_columns,
        jnp.asarray(signs),
        aug_table,
        jnp.asarray(np.stack([spread_high, spread_low])),
    )
    y_block = NY // bands
    total = devices * slots
    result = pl.pallas_call(
        functools.partial(finish_kernel, bands, groups),
        in_specs=[vmem],
        out_specs=vmem,
        out_shape=jax.ShapeDtypeStruct((planes, y_block, 2, NX), F32),
        scratch_shapes=[
            pltpu.VMEM((2, 2 * total, 512), BF16),
            pltpu.VMEM((lanes, total), F32),
            pltpu.VMEM((2, up(y_block, 16), total), F32),
        ],
        name="finish",
    )(received.reshape(total, lanes))
    return result.transpose(2, 0, 1, 3)


def solution(mesh):
    in_specs = (
        P(None, "band", "ga"),
        P("band"),
        P(None, "ga"),
        P(None, "ga"),
        P(),
        P(),
        P(None, ("band", "ga")),
        P(("band", "ga")),
    )
    out_specs = P(None, "ga", "band", None)
    return jax.shard_map(
        on_device, mesh=mesh, in_specs=in_specs, out_specs=out_specs, check_vma=False
    )
```

time: 150 us -> 56 us (0.37)
  waiting for transfers between devices: 43 us -> 0 us
  blocking collectives: 42 us -> 0 us
  Pallas kernels: 19.3 us -> 55.9 us
  between operations: 13.7 us -> 0.01 us
  local copies, waits for them, and re-layouts: 13.2 us -> 0 us
  other arithmetic: 10.2 us -> 0 us
  matrix products: 4.89 us -> 0 us
  starting transfers between devices: 3.34 us -> 0 us
    reduce_scatter x1 -> x0, waiting for transfers between devices: 38.3 us -> none  [on_device(): own = lax.psum_scatter(pieces, 'ga', scatter_dimension=1, tiled=True)]
    pallas_call x2, Pallas kernels: 19.3 us -> 55.9 us  [the longest x1 43.7 us: on_device(): pl.pallas_call(functools.partial(mega_kernel, bands, groups), in_specs=[v...]
    all_gather x2 -> x0, blocking collectives: 23 us -> none  [the longest x1 13.7 us: on_device(): lax.all_gather(received.reshape(groups * slots, -1), 'band', axis=0, tile...]
    psum x1 -> x0, blocking collectives: 19 us -> none  [on_device(): lax.psum(partial_value, 'band')]
    dot_general x4 -> x0, matrix products: 4.89 us -> none  [the longest x1 1.68 us: finish(): out_re = lax.dot_general(amp, wave_re, dims, precision=lax.Precision.HIGH)]
    another operation x4 -> x0, local copies, waits for them, and re-layouts: 4.68 us -> none  [the longest x1 4.42 us: finish(): return jnp.stack([out_re, out_im])]
    all_to_all x1 -> x0, waiting for transfers between devices: 4.67 us -> none  [on_device(): lax.all_to_all(packed, 'ga', split_axis=0, concat_axis=0, tiled=True)]
    all_to_all x1 -> x0, starting transfers between devices: 3.34 us -> none  [on_device(): lax.all_to_all(packed, 'ga', split_axis=0, concat_axis=0, tiled=True)]
  transfers between devices with their start and end apart: 2 -> 0, of which waited for: 2 -> 0; matrix products, arithmetic and copies ran while one was open for 1% -> 0% of each run, Pallas kernels for 0% -> 0%
where the time goes in v3:
time: 56 us; the launch traced here: 55.9 us
  Pallas kernels  55.9 us (100%)
    pallas_call x1, Pallas kernels, on_device(): pl.pallas_call(functools.partial(mega_kernel, bands, groups), in_specs=[v...  43.7 us
    pallas_call x1, Pallas kernels, on_device(): pl.pallas_call(functools.partial(finish_kernel, bands, groups), in_specs=...  12.2 us

profile of v3, /device:TPU:0, one launch (start us, length us, event | category | flops | bytes accessed | tf_op | source)
XLA Modules:
  0.0 55.9 jit_solution(11310218411692830441)
XLA Ops:
  0.0 43.7 %slots.1 = f32[32,8,128]{2,1,0:T(8,128)} custom-call(bf16[2,32,1024]{2,1,0:T(8,128)(2,1)} %waves_ref.1, f32[1,32]{1,0:T(1,128)} %bitcast.6, f32[72,1024]{1,0:T(8,128)} %beta_ref.1, s32[3,1024]{1,0:T(4,128)} %miller_ref.1, s32[1,256]{1,0:T(1,128)} %bitcast.5, s32[3,256]{1,0:T(4,128)} %site_ref.1, s32[8]{0:T(128)} %columns_ref.1, ...), custom_call_target="tpu_custom_call" | custom-call | tf_op jit(solution)/shard_map/slots/pallas_call | solution.py:453
  43.7 12.2 %finish.1 = f32[28,60,2,240]{3,2,1,0:T(2,128)} custom-call(f32[256,128]{1,0:T(8,128)} %bitcast.4), custom_call_target="tpu_custom_call" | custom-call | tf_op jit(solution)/shard_map/finish/pallas_call | solution.py:504

commit v4 on v3

--- a/solution.py
+++ b/solution.py
@@ -368,45 +368,53 @@
         stick_copy(step, place).wait_send()
 
 
-def finish_kernel(bands, groups, received_ref, out_ref, table_ref, turned_ref, angle_ref):
+def finish_kernel(bands, planes, received_ref, out_ref, table_ref, turned_ref, angle_ref, amp_ref):
     total, lanes = received_ref.shape
-    planes = out_ref.shape[0]
+    batch = out_ref.shape[0]
     y_block = out_ref.shape[1]
     y_pad = angle_ref.shape[1]
     band = lax.axis_index("band")
-    received = received_ref[...]
-    turned = jnp.swapaxes(received, 0, 1)
-    turned_ref[...] = turned
-    column_row = turned[2 * planes : 2 * planes + 1, :]
-    live_row = column_row >= 0.0
-    x_row = jnp.floor((column_row + 0.5) * (1.0 / NY))
-    y_row = column_row - x_row * NY
-    y_values = lax.broadcasted_iota(jnp.int32, (y_pad, total), 0) + band * y_block
-    cos_y, sin_y = turn_cos_sin(y_values.astype(F32) * y_row, NY)
-    angle_ref[0] = jnp.where(live_row, cos_y, 0.0)
-    angle_ref[1] = jnp.where(live_row, sin_y, 0.0)
-    column = received[:, 2 * planes : 2 * planes + 1]
-    owner = lax.broadcasted_iota(jnp.int32, (total, 1), 0) // (total // bands)
-    x = jnp.floor((column + 0.5) * (1.0 / NY)) + owner.astype(F32) * (NX // bands)
-    x_values = lax.broadcasted_iota(jnp.int32, (total, 256), 1).astype(F32)
-    cos_x, sin_x = turn_cos_sin(x * x_values, NX)
-    for part, value in enumerate(split(cos_x)):
-        table_ref[part, 0:total, 0:256] = value
-        table_ref[part, total : 2 * total, 256:512] = value
-    for part, value in enumerate(split(sin_x)):
-        table_ref[part, 0:total, 256:512] = value
-        table_ref[part, total : 2 * total, 0:256] = -value
-
-    @pl.loop(0, planes)
-    def _(z):
-        real = turned_ref[pl.ds(z, 1), :]
-        imag = turned_ref[pl.ds(planes + z, 1), :]
+    group = pl.program_id(0)
+
+    @pl.when(group == 0)
+    def _():
+        received = received_ref[...]
+        turned = jnp.swapaxes(received, 0, 1)
+        turned_ref[...] = turned
+        column_row = turned[2 * planes : 2 * planes + 1, :]
+        live_row = column_row >= 0.0
+        x_row = jnp.floor((column_row + 0.5) * (1.0 / NY))
+        y_row = column_row - x_row * NY
+        y_values = lax.broadcasted_iota(jnp.int32, (y_pad, total), 0) + band * y_block
+        cos_y, sin_y = turn_cos_sin(y_values.astype(F32) * y_row, NY)
+        angle_ref[0] = jnp.where(live_row, cos_y, 0.0)
+        angle_ref[1] = jnp.where(live_row, sin_y, 0.0)
+        column = received[:, 2 * planes : 2 * planes + 1]
+        owner = lax.broadcasted_iota(jnp.int32, (total, 1), 0) // (total // bands)
+        x = jnp.floor((column + 0.5) * (1.0 / NY)) + owner.astype(F32) * (NX // bands)
+        x_values = lax.broadcasted_iota(jnp.int32, (total, 256), 1).astype(F32)
+        cos_x, sin_x = turn_cos_sin(x * x_values, NX)
+        for part, value in enumerate(split(cos_x)):
+            table_ref[part, 0:total, 0:256] = value
+            table_ref[part, total : 2 * total, 256:512] = value
+        for part, value in enumerate(split(sin_x)):
+            table_ref[part, 0:total, 256:512] = value
+            table_ref[part, total : 2 * total, 0:256] = -value
+
+    for k in range(batch):
+        real = turned_ref[pl.ds(group * batch + k, 1), :]
+        imag = turned_ref[pl.ds(planes + group * batch + k, 1), :]
         cosine, sine = angle_ref[0], angle_ref[1]
-        amp = jnp.concatenate([real * cosine - imag * sine, real * sine + imag * cosine], axis=1).astype(BF16)
-        result = jnp.dot(amp, table_ref[0], preferred_element_type=F32)
-        result = result + jnp.dot(amp, table_ref[1], preferred_element_type=F32)
-        out_ref[z, :, 0, :] = result[:y_block, 0:NX]
-        out_ref[z, :, 1, :] = result[:y_block, 256 : 256 + NX]
+        row = k * y_pad
+        amp_ref[row : row + y_pad, 0:total] = (real * cosine - imag * sine).astype(BF16)
+        amp_ref[row : row + y_pad, total : 2 * total] = (real * sine + imag * cosine).astype(BF16)
+    amp = amp_ref[...]
+    for part in range(2):
+        lane = slice(256 * part, 256 * part + 256)
+        result = jnp.dot(amp, table_ref[0, :, lane], preferred_element_type=F32)
+        result = result + jnp.dot(amp, table_ref[1, :, lane], preferred_element_type=F32)
+        for k in range(batch):
+            out_ref[k, :, part, :] = result[k * y_pad : k * y_pad + y_block, 0:NX]
 
 
 def on_device(
@@ -501,15 +509,19 @@
     )
     y_block = NY // bands
     total = devices * slots
+    batch = math.gcd(planes, 7)
+    y_pad = up(y_block, 16)
     result = pl.pallas_call(
-        functools.partial(finish_kernel, bands, groups),
-        in_specs=[vmem],
-        out_specs=vmem,
+        functools.partial(finish_kernel, bands, planes),
+        grid=(planes // batch,),
+        in_specs=[pl.BlockSpec((total, lanes), lambda g: (0, 0))],
+        out_specs=pl.BlockSpec((batch, y_block, 2, NX), lambda g: (g, 0, 0, 0)),
         out_shape=jax.ShapeDtypeStruct((planes, y_block, 2, NX), F32),
         scratch_shapes=[
             pltpu.VMEM((2, 2 * total, 512), BF16),
             pltpu.VMEM((lanes, total), F32),
-            pltpu.VMEM((2, up(y_block, 16), total), F32),
+            pltpu.VMEM((2, y_pad, total), F32),
+            pltpu.VMEM((batch * y_pad, 2 * total), BF16),
         ],
         name="finish",
     )(received.reshape(total, lanes))

time: 56 us -> 49.5 us (0.88)
  Pallas kernels: 55.9 us -> 49.4 us
    pallas_call x1, Pallas kernels: 12.2 us -> 5.66 us  [on_device(): pl.pallas_call(functools.partial(finish_kernel, bands, planes), grid=(pla...]
where the time goes in v4:
time: 49.5 us; the launch traced here: 49.4 us
  Pallas kernels  49.4 us (100%)
    pallas_call x1, Pallas kernels, on_device(): pl.pallas_call(functools.partial(mega_kernel, bands, groups), in_specs=[v...  43.7 us
    pallas_call x1, Pallas kernels, on_device(): pl.pallas_call(functools.partial(finish_kernel, bands, planes), grid=(pla...  5.66 us

profile of v4, /device:TPU:0, one launch (start us, length us, event | category | flops | bytes accessed | tf_op | source)
XLA Modules:
  0.0 49.4 jit_solution(2429268860506742717)
XLA Ops:
  0.0 43.7 %slots.1 = f32[32,8,128]{2,1,0:T(8,128)} custom-call(bf16[2,32,1024]{2,1,0:T(8,128)(2,1)} %waves_ref.1, f32[1,32]{1,0:T(1,128)} %bitcast.6, f32[72,1024]{1,0:T(8,128)} %beta_ref.1, s32[3,1024]{1,0:T(4,128)} %miller_ref.1, s32[1,256]{1,0:T(1,128)} %bitcast.5, s32[3,256]{1,0:T(4,128)} %site_ref.1, s32[8]{0:T(128)} %columns_ref.1, ...), custom_call_target="tpu_custom_call" | custom-call | tf_op jit(solution)/shard_map/slots/pallas_call | solution.py:461
  43.7 5.7 %finish.1 = f32[28,60,2,240]{3,2,1,0:T(2,128)} custom-call(f32[256,128]{1,0:T(8,128)} %bitcast.4), custom_call_target="tpu_custom_call" | custom-call | tf_op jit(solution)/shard_map/finish/pallas_call | solution.py:514

commit v5 on v4

--- a/solution.py
+++ b/solution.py
@@ -63,7 +63,7 @@
         def _(step):
             pl.semaphore_signal(barrier, inc=1, device_id=device_of(step), device_id_type=MESH)
 
-    pl.semaphore_wait(barrier, peers)
+    return lambda: pl.semaphore_wait(barrier, peers)
 
 
 def up(value, unit):
@@ -143,7 +143,7 @@
         other = lax.rem(place + step, devices)
         return other // groups, lax.rem(other, groups)
 
-    greet(devices - 1, [(devices, peer)])
+    all_here = greet(devices - 1, [(devices, peer)])
 
     small_ref[...] = jnp.zeros_like(small_ref)
     small_ref[0:1, :] = site_ref[0:1, :].astype(F32) * STEP_X
@@ -201,6 +201,11 @@
             rows_ref[...], wave_ref[...], (((1,), (1,)), ((), ())), preferred_element_type=F32
         )
         send_ref[index] = result.reshape(HALF, block, cols)
+
+        @pl.when(step == 0)
+        def _():
+            all_here()
+
         for part in range(ratio):
             target = index * ratio + part
 

time: 49.5 us -> 48.2 us (0.974)
  Pallas kernels: 49.4 us -> 48 us
    pallas_call x1, Pallas kernels: 43.7 us -> 42.4 us  [on_device(): pl.pallas_call(functools.partial(mega_kernel, bands, groups), in_specs=[v...]
where the time goes in v5:
time: 48.2 us; the launch traced here: 48.1 us
  Pallas kernels  48 us (100%)
    pallas_call x1, Pallas kernels, on_device(): pl.pallas_call(functools.partial(mega_kernel, bands, groups), in_specs=[v...  42.4 us
    pallas_call x1, Pallas kernels, on_device(): pl.pallas_call(functools.partial(finish_kernel, bands, planes), grid=(pla...  5.66 us

profile of v5, /device:TPU:0, one launch (start us, length us, event | category | flops | bytes accessed | tf_op | source)
XLA Modules:
  0.0 48.1 jit_solution(8587447175069220448)
XLA Ops:
  0.0 42.4 %slots.1 = f32[32,8,128]{2,1,0:T(8,128)} custom-call(bf16[2,32,1024]{2,1,0:T(8,128)(2,1)} %waves_ref.1, f32[1,32]{1,0:T(1,128)} %bitcast.6, f32[72,1024]{1,0:T(8,128)} %beta_ref.1, s32[3,1024]{1,0:T(4,128)} %miller_ref.1, s32[1,256]{1,0:T(1,128)} %bitcast.5, s32[3,256]{1,0:T(4,128)} %site_ref.1, s32[8]{0:T(128)} %columns_ref.1, ...), custom_call_target="tpu_custom_call" | custom-call | tf_op jit(solution)/shard_map/slots/pallas_call | solution.py:466
  42.4 5.7 %finish.1 = f32[28,60,2,240]{3,2,1,0:T(2,128)} custom-call(f32[256,128]{1,0:T(8,128)} %bitcast.4), custom_call_target="tpu_custom_call" | custom-call | tf_op jit(solution)/shard_map/finish/pallas_call | solution.py:519
